TPU v7x, 256 devices: a whole 4x4x8 slice. The times are simulated.
256 devices in a mesh: row: 8 (over x, core), col: 8 (over z), depth: 4 (over y).
Axes of the slice: x: 4, y: 4, z: 8, core: 2. Of those that a mesh axis runs over, the one named last changes fastest.
Arguments:
- x_blocks: bfloat16 [256, 4, 256, 256], P(('row', 'col'), 'depth'), may hold values from -0.25 to 0.25
- x_columns: int32 [256, 4], P(('row', 'col'), 'depth'), may hold values from 0 to 255, as said below
- h_blocks: bfloat16 [256, 4, 256, 256], P(('row', 'col')), may hold values from -6 to 6
- h_columns: int32 [256, 4], P(('row', 'col')), may hold values from 0 to 255, as said below
- p_columns: int32 [256, 4], P(('row', 'col')), may hold values from 0 to 255, as said below
- q_columns: int32 [256, 4], P(('row', 'col')), may hold values from 0 to 255, as said below
Outputs:
- product_p: bfloat16 [256, 4, 256, 256], P(('row', 'col'), 'depth')
- product_q: bfloat16 [256, 4, 256, 256], P(('row', 'col'), 'depth')
Inputs may be any that keep to these rules, and one draw needn't show every extreme that they name: `x_columns`: row i holds 4 distinct block columns (i + o) mod 256 with -2 <= o <= 2. `h_columns`: row i holds 4 distinct block columns (i + o) mod 256 with -2 <= o <= 2. `p_columns`: row i holds 4 distinct block columns (i + o) mod 256 with -4 <= o <= 4. `q_columns`: row i holds 4 distinct block columns (i + o) mod 256 with -6 <= o <= 6.
All inputs are finite; a program needn't handle non-finite values.
Results may differ from a plain program's by a relative error of at most 0.0049.
Values may be sent and summed in bfloat16 or wider, within the bound.
No kernel may reach another device: no remote copies, remote signals or barrier semaphores. Data moves between devices by JAX's collectives and lax.ppermute only.
A program may use at most 64 MiB of HBM per device.

v0:
```python
import functools

import jax
import jax.numpy as jnp
from jax import lax
from jax.experimental import pallas as pl
from jax.experimental.pallas import tpu as pltpu
from jax.sharding import PartitionSpec as P


REACH = 2
PAD = 16
BF16, F32, I32 = jnp.bfloat16, jnp.float32, jnp.int32


ANY = pl.BlockSpec(memory_space=pl.ANY)
SMEM = pl.BlockSpec(memory_space=pltpu.SMEM)
VMEM = pl.BlockSpec(memory_space=pltpu.VMEM)
HBM = pl.BlockSpec(memory_space=pltpu.HBM)


def low_half(shape):
    return lax.broadcasted_iota(I32, shape, 1) < 64


def swapped(tile):
    return pltpu.roll(tile.astype(F32), 64, 1).astype(tile.dtype)


def vmem(x):
    return pltpu.with_memory_space_constraint(x, pltpu.VMEM)


def hbm(x):
    return pltpu.with_memory_space_constraint(x, pltpu.HBM)


def copies(pairs, sems):
    made = [pltpu.make_async_copy(a, b, sems.at[n]) for n, (a, b) in enumerate(pairs)]
    for copy in made:
        copy.start()
    return made


def pack_kernel(x_columns, h_columns, x, h, x_low, x_high, h_up, h_down, xc, hc, sems):
    cut, size = x_low.shape
    tail = x_high.shape[0] - PAD
    edge = h_up.shape[0] - PAD
    rows, slots = hc.shape
    d, straight = lax.axis_index("depth"), slots - 1
    small = copies([(x_columns, xc), (h_columns, hc)], sems.at[pl.ds(14, 2)])
    moves = copies(
        [
            (x.at[pl.ds(0, cut)], x_low),
            (x.at[pl.ds(cut, tail)], x_high.at[pl.ds(0, tail)]),
        ]
        + [
            (
                h.at[pl.ds(pl.multiple_of(((start + r) * slots + lax.rem(d + way * n + slots, slots)) * size, size), size)],
                out.at[pl.ds((r * straight + n) * size, size)],
            )
            for out, start, way in ((h_up, rows - REACH, 1), (h_down, 0, -1))
            for r in range(REACH)
            for n in range(straight)
        ],
        sems,
    )
    shape = (PAD, size)
    row, lane = lax.broadcasted_iota(I32, shape, 0), lax.broadcasted_iota(I32, shape, 1)
    for move in small:
        move.wait()
    table = jnp.zeros(shape, I32)
    for r in range(rows):
        table = jnp.where(row == r, xc[0, r], table)
    x_high[tail:, :] = table.astype(F32).astype(BF16)
    for out, start in ((h_up, rows - REACH), (h_down, 0)):
        table = jnp.zeros(shape, I32)
        for r in range(REACH):
            for m in range(slots):
                table = jnp.where((row == r) & (lane == m), hc[start + r, m], table)
        out[edge:, :] = table.astype(F32).astype(BF16)
    for move in moves:
        move.wait()


def pack(x_blocks, x_columns, h_blocks, h_columns):
    rows, slots, size, _ = h_blocks.shape
    x, h = x_blocks.reshape(-1, size), h_blocks.reshape(-1, size)
    half = rows // 2 * size
    edge = pltpu.VMEM((REACH * (slots - 1) * size + PAD, size), BF16)
    return pl.pallas_call(
        pack_kernel,
        in_specs=[HBM] * 4,
        out_specs=[VMEM] * 4,
        out_shape=[
            pltpu.VMEM((half, size), BF16),
            pltpu.VMEM((x.shape[0] - half + PAD, size), BF16),
            edge,
            edge,
        ],
        scratch_shapes=[
            pltpu.SMEM((1, rows), I32),
            pltpu.SMEM((rows, slots), I32),
            pltpu.SemaphoreType.DMA((16,)),
        ],
        compiler_params=pltpu.CompilerParams(vmem_limit_bytes=8 << 20),
        name="pack",
    )(*[hbm(a) for a in (x_columns.T, h_columns, x, h)])


def slice_kernel(a_low, a_high, b_low, b_high, out):
    d = lax.axis_index("depth")
    tile = pl.ds(pl.multiple_of(d // 2 * 128, 128), 128)
    cut = a_low.shape[0]
    for upper in range(2):

        @pl.when(d % 2 == upper)
        def _():
            for left, right, rows in ((a_low, b_low, slice(0, cut)), (a_high, b_high, slice(cut, None))):
                a, b = left[:, tile], right[:, tile]
                a, b = (swapped(a), b) if upper else (a, swapped(b))
                out[rows, :] = jnp.where(low_half(a.shape), a, b)


def column_slices(payloads):
    low, high = payloads[:2]
    return pl.pallas_call(
        slice_kernel,
        in_specs=[VMEM] * 4,
        out_specs=VMEM,
        out_shape=pltpu.VMEM((low.shape[0] + high.shape[0], 128), BF16),
        compiler_params=pltpu.CompilerParams(vmem_limit_bytes=8 << 20),
        name="column_slices",
    )(*[vmem(x) for x in payloads])


def first_slot_kernel(lo, hi, out_lo, out_hi):
    size = lo.shape[1]
    step = (lo.shape[0] - PAD) // REACH
    for source, out in ((lo, out_lo), (hi, out_hi)):
        for r in range(REACH):
            out[r * size : r * size + size, :] = source[r * step : r * step + size, :]


def first_slots(lo, hi):
    size = lo.shape[1]
    return pl.pallas_call(
        first_slot_kernel,
        in_specs=[VMEM] * 2,
        out_specs=[VMEM] * 2,
        out_shape=[pltpu.VMEM((REACH * size, size), BF16)] * 2,
        compiler_params=pltpu.CompilerParams(vmem_limit_bytes=4 << 20),
        name="first_slots",
    )(vmem(lo), vmem(hi))


def table_to_scalars(tables, tabv, tab, sem):
    for n, table in enumerate(tables):
        tabv[8 * n : 8 * n + 8, :] = table.astype(F32).astype(I32)
    move = pltpu.make_async_copy(tabv, tab, sem)
    move.start()
    move.wait()


def x_tables(xs):
    return [x[x.shape[0] - PAD : x.shape[0] - PAD + 8, :128] for x in xs[1::2]]


def x_row(xs, k, i):
    cut, size = xs[0].shape
    at = i * size % cut
    return xs[2 * k + i * size // cut][at : at + size, :]


def own_block(column, first, all_rows, want, hc, h, zero):
    rows, slots = hc.shape
    size = h.shape[1]
    j = lax.rem(column - first + all_rows, all_rows)
    row = jnp.minimum(j, rows - 1)
    pick, found = jnp.int32(0), jnp.bool_(False)
    for m in range(slots):
        match = (hc[row, m] == want) & (j < rows)
        pick = jnp.where(match, m, pick)
        found = found | match
    spot = pl.multiple_of((row * slots + pick) * size, size)
    return jnp.where(found, h[pl.ds(spot, size), :], zero)


def near_kernel(rows, all_rows, pc, hc, *refs):
    *xs, h, total, tabv, tab, sem = refs
    size = h.shape[1]
    slots = pc.shape[1]
    first = lax.axis_index(("row", "col")) * rows
    table_to_scalars(x_tables(xs), tabv, tab, sem)
    zero = jnp.zeros((size, size), BF16)
    for i in range(rows):
        for p in range(slots):
            acc = jnp.zeros((size, size), F32)
            for k in range(len(xs) // 2):
                block = own_block(tab[8 * k + i, 0], first, all_rows, pc[i, p], hc, h, zero)
                acc += jnp.dot(x_row(xs, k, i), block, preferred_element_type=F32)
            total[i * slots + p] = acc


def near_terms(pc, hc, xs, h, all_rows):
    rows, slots = pc.shape
    size = h.shape[-1]
    return pl.pallas_call(
        functools.partial(near_kernel, rows, all_rows),
        in_specs=[SMEM] * 2 + [VMEM] * (len(xs) + 1),
        out_specs=VMEM,
        out_shape=pltpu.VMEM((rows * slots, size, size), F32),
        scratch_shapes=[
            pltpu.VMEM((4 * len(xs), 128), I32),
            pltpu.SMEM((4 * len(xs), 128), I32),
            pltpu.SemaphoreType.DMA,
        ],
        cost_estimate=pl.CostEstimate(
            flops=rows * slots * len(xs) * size**3, bytes_accessed=9 << 20, transcendentals=0
        ),
        compiler_params=pltpu.CompilerParams(vmem_limit_bytes=8 << 20),
        name="near_terms",
    )(pc, hc, *[vmem(x) for x in xs], vmem(h.reshape(-1, size)))


def far_kernel(rows, all_rows, pc, *refs):
    *xs, lo, hi, lo_side, hi_side, total, full, mine, tabv, tab, sem = refs
    size = lo.shape[1]
    slots = pc.shape[1]
    edge = lo.shape[0] - PAD
    d, first = lax.axis_index("depth"), lax.axis_index(("row", "col")) * rows
    table_to_scalars(
        x_tables(xs) + [e[edge : edge + 8, :128] for e in (lo, hi)], tabv, tab, sem
    )
    zero = jnp.zeros((size, size), BF16)
    for i in range(rows):
        far = [(32 + r, lo, lo_side, r, 1, r - REACH) for r in range(REACH) if r - REACH >= i - REACH]
        far += [(40 + r, hi, hi_side, r, -1, rows + r) for r in range(REACH) if rows + r <= i + REACH]
        lefts = []
        for *_, j in far:
            column = lax.rem(first + j + all_rows, all_rows)
            left = zero
            for k in range(4):
                left = jnp.where(tab[8 * k + i, 0] == column, x_row(xs, k, i), left)
            lefts.append(left)
        for p in range(slots):
            want = pc[i, p]
            acc = total[i * slots + p]
            for left, (at, straight, side, r, way, _) in zip(lefts, far):
                pick, found = jnp.int32(0), jnp.bool_(False)
                for m in range(slots):
                    match = tab[at, m] == want
                    pick = jnp.where(match, m, pick)
                    found = found | match
                n = lax.rem(way * (pick - d) + slots, slots)
                spot = (r * (slots - 1) + jnp.minimum(n, slots - 2)) * size
                block = jnp.where(
                    n < slots - 1,
                    straight[pl.ds(pl.multiple_of(spot, size), size), :],
                    side[r * size : r * size + size, :],
                )
                acc += jnp.dot(left, jnp.where(found, block, zero), preferred_element_type=F32)
            full[i * slots + p] = acc.astype(BF16)
        mine[i] = full[i * slots + d]


def far_terms(pc, xs, edges, total, all_rows):
    rows, slots = pc.shape
    size = total.shape[-1]
    return pl.pallas_call(
        functools.partial(far_kernel, rows, all_rows),
        in_specs=[SMEM] + [VMEM] * 13,
        out_specs=[VMEM, VMEM],
        out_shape=[
            pltpu.VMEM((rows * slots, size, size), BF16),
            jax.ShapeDtypeStruct((rows, size, size), BF16),
        ],
        scratch_shapes=[
            pltpu.VMEM((48, 128), I32),
            pltpu.SMEM((48, 128), I32),
            pltpu.SemaphoreType.DMA,
        ],
        cost_estimate=pl.CostEstimate(
            flops=2 * 24 * size**3, bytes_accessed=9 << 20, transcendentals=0
        ),
        compiler_params=pltpu.CompilerParams(vmem_limit_bytes=8 << 20),
        name="far_terms",
    )(pc, *[vmem(x) for x in (*xs, *edges, total)])


def q_kernel(rows, all_rows, pc, qc, lo_a, own_a, hi_a, lo_b, own_b, hi_b, full, s0, s1, s2, s3, tiles, tabv, tab, res, sem):
    size = full.shape[1]
    body = rows * size
    slots = pc.shape[1]
    raw = ((lo_a, lo_b), (own_a, own_b), (hi_a, hi_b))
    d, first = lax.axis_index("depth"), lax.axis_index(("row", "col")) * rows
    for n in range(3):
        for t in range(2):
            part = raw[n][t][body : body + 8, :]
            tabv[8 * n : 8 * n + 8, 128 * t : 128 * t + 128] = part.astype(F32).astype(I32)
    move = pltpu.make_async_copy(tabv, tab, sem)
    move.start()
    empty = 12 * slots * size
    tiles[pl.ds(empty, size), :] = jnp.zeros((size, 128), BF16)
    for n in range(3):
        for r in range(rows):
            for t in range(2):
                tile = raw[n][t][r * size : r * size + size, :]
                base = (((n * rows + r) * 2 + t) * 2) * size
                tiles[base : base + size, :] = tile
                tiles[base + size : base + 2 * size, :] = swapped(tile)
    move.wait()
    mask = low_half((size, 128))

    for i in range(rows):
        acc = jnp.zeros((size, size), F32)
        for p in range(slots):
            j = lax.rem(pc[i, p] - first + rows + all_rows, all_rows)
            tab_row = 8 * (j // rows) + j % rows
            picks = []
            for q in range(slots):
                half = (q + i) % 2
                pick = jnp.int32(empty)
                for m in range(slots):
                    spot = (j * 4 + (m // 2) * 2 + (m % 2 != half)) * size
                    pick = jnp.where(tab[tab_row, 64 * m] == qc[i, q], spot, pick)
                picks.append(tiles[pl.ds(pl.multiple_of(pick, size), size), :])
            pairs = [(picks[0], picks[1]), (picks[2], picks[3])]
            if i % 2:
                pairs = [(b, a) for a, b in pairs]
            right = jnp.concatenate([jnp.where(mask, a, b) for a, b in pairs], axis=1)
            acc += jnp.dot(full[i * slots + p], right, preferred_element_type=F32)
        value = acc.astype(BF16)
        res[2 * i] = value[:, :128]
        res[2 * i + 1] = value[:, 128:]
    for o, out in enumerate((s0, s1, s2, s3)):
        q = lax.rem(d + o, 4)
        even = mask == (q % 2 == 0)
        for e in range(rows // 2):
            out[e * size : e * size + size, :] = jnp.where(
                even, res[4 * e + q // 2], res[4 * e + 2 + q // 2]
            )


def q_product(pc, qc, pieces, full, all_rows):
    rows, slots = pc.shape
    size = full.shape[1]
    return pl.pallas_call(
        functools.partial(q_kernel, rows, all_rows),
        in_specs=[SMEM] * 2 + [VMEM] * 7,
        out_specs=[VMEM] * 4,
        out_shape=[pltpu.VMEM((rows // 2 * size, 128), BF16)] * 4,
        scratch_shapes=[
            pltpu.VMEM(((12 * slots + 1) * size, 128), BF16),
            pltpu.VMEM((24, size), I32),
            pltpu.SMEM((24, size), I32),
            pltpu.VMEM((2 * rows, size, 128), BF16),
            pltpu.SemaphoreType.DMA,
        ],
        cost_estimate=pl.CostEstimate(
            flops=2 * rows * slots * size**3, bytes_accessed=5 << 20, transcendentals=0
        ),
        compiler_params=pltpu.CompilerParams(vmem_limit_bytes=24 << 20),
        name="q_product",
    )(pc, qc, *[vmem(x) for x in (*pieces, full)])


def join_kernel(t0, t1, t2, t3, out, held):
    size, d = out.shape[1], lax.axis_index("depth")
    for o, t in enumerate((t0, t1, t2, t3)):
        held[lax.rem(d - o + 4, 4)] = t[...]
    mask = low_half((size, 128))
    for side in range(2):

        @pl.when(d % 2 == side)
        def _():
            for i in range(out.shape[0]):
                rows = slice(i // 2 * size, i // 2 * size + size)
                for t in range(2):
                    a, b = held[2 * t, rows], held[2 * t + 1, rows]
                    if (side + i) % 2 == 0:
                        b = swapped(b)
                    else:
                        a = swapped(a)
                    out[i, :, 128 * t : 128 * t + 128] = jnp.where(mask, a, b)


def join(parts, rows, size):
    return pl.pallas_call(
        join_kernel,
        in_specs=[VMEM] * 4,
        out_specs=VMEM,
        out_shape=jax.ShapeDtypeStruct((rows, size, size), BF16),
        scratch_shapes=[pltpu.VMEM((4, *parts[0].shape), BF16)],
        compiler_params=pltpu.CompilerParams(vmem_limit_bytes=8 << 20),
        name="join",
    )(*[vmem(x) for x in parts])


def local(x_blocks, x_columns, h_blocks, h_columns, p_columns, q_columns):
    rows, _, size, _ = x_blocks.shape
    groups = lax.axis_size(("row", "col"))
    depth = lax.axis_size("depth")
    all_rows = rows * groups
    up = [(g, (g + 1) % groups) for g in range(groups)]
    down = [(b, a) for a, b in up]

    def turn(x, o):
        return lax.ppermute(x, "depth", [(s, (s + o) % depth) for s in range(depth)])

    def shift(x, pairs):
        return lax.ppermute(x, ("row", "col"), pairs)

    x_low, x_high, h_up, h_down = pack(x_blocks, x_columns, h_blocks, h_columns)
    h_lo, h_hi = shift(h_up, up), shift(h_down, down)
    low_one, high_three = turn(x_low, 1), turn(x_high, 3)
    high_one, low_three = turn(x_high, 1), turn(x_low, 3)
    low_two, high_two = turn(low_one, 1), turn(high_three, 3)
    xs = [x_low, x_high, low_one, high_one, low_three, high_three, low_two, high_two]

    a = column_slices(xs[:4])
    a_lo, a_hi = shift(a, up), shift(a, down)
    send_lo, send_hi = first_slots(h_lo, h_hi)
    edges = [h_lo, h_hi, turn(send_lo, 1), turn(send_hi, 3)]
    b = column_slices(xs[4:])
    b_lo, b_hi = shift(b, up), shift(b, down)
    total = near_terms(p_columns, h_columns, xs, h_blocks, all_rows)
    full, mine = far_terms(p_columns, xs, edges, total, all_rows)
    pieces = (a_lo, a, a_hi, b_lo, b, b_hi)
    parts = q_product(p_columns, q_columns, pieces, full, all_rows)
    parts = [parts[0]] + [turn(parts[o], o) for o in range(1, depth)]
    product_q = join(parts, rows, size)
    return mine[:, None], product_q[:, None]


def solution(mesh):
    in_specs = (
        P(("row", "col"), "depth", None, None),
        P(("row", "col"), "depth"),
        P(("row", "col"), None, None, None),
        P(("row", "col"), None),
        P(("row", "col"), None),
        P(("row", "col"), None),
    )
    out_specs = (P(("row", "col"), "depth", None, None), P(("row", "col"), "depth", None, None))
    return jax.shard_map(local, mesh=mesh, in_specs=in_specs, out_specs=out_specs, check_vma=False)
```

profile of v0, /device:TPU:7, one launch (start us, length us, event | category | flops | bytes accessed | tf_op | source)
XLA Modules:
  0.0 63.6 jit_solution(6354210297873806960)
XLA Ops:
  0.6 1.6 %pack.1 = (bf16[512,256]{1,0:T(8,128)(2,1)S(1)}, bf16[528,256]{1,0:T(8,128)(2,1)S(1)}, bf16[1552,256]{1,0:T(8,128)(2,1)S(1)}, bf16[1552,256]{1,0:T(8,128)(2,1)S(1)}) custom-call(s32[1,4]{1,0:T(1,128)} %bitcast.13, s32[4,4]{1,0:T(4,128)} %hc.1, bf16[1024,256]{1,0:T(8,128)(2,1)} %bitcast.11, bf16[4096,256]{1,0:T(8,128)(2,1)} %bitcast.9), custom_call_target="tpu_custom_call" | custom-call | tf_op jit(solution)/shard_map/pack/pallas_call | solution.py:91
  2.3 1.7 %collective-permute-start.6 = (bf16[1552,256]{1,0:T(8,128)(2,1)S(1)}, bf16[1552,256]{1,0:T(8,128)(2,1)S(1)}, u32[]{:S(2)}, u32[]{:S(2)}) collective-permute-start(bf16[1552,256]{1,0:T(8,128)(2,1)S(1)} %get-tuple-element.16), channel_id=1, source_target_pairs={{0,4},{4,8},{8,12},{12,16},{16,20},{20,24},{24,28},{28,32},{32,36}... | collective-permute-start | bytes 2383880 | tf_op jit(solution)/shard_map/ppermute | solution.py:412
  4.0 4.6 %collective-permute-start.7 = (bf16[1552,256]{1,0:T(8,128)(2,1)S(1)}, bf16[1552,256]{1,0:T(8,128)(2,1)S(1)}, u32[]{:S(2)}, u32[]{:S(2)}) collective-permute-start(bf16[1552,256]{1,0:T(8,128)(2,1)S(1)} %get-tuple-element.17), channel_id=1, source_target_pairs={{4,0},{8,4},{12,8},{16,12},{20,16},{24,20},{28,24},{32,28},{36,32}... | collective-permute-start | bytes 2383880 | tf_op jit(solution)/shard_map/ppermute | solution.py:412
  8.6 2.7 %collective-permute-start.3 = (bf16[528,256]{1,0:T(8,128)(2,1)S(1)}, bf16[528,256]{1,0:T(8,128)(2,1)S(1)}, u32[]{:S(2)}, u32[]{:S(2)}) collective-permute-start(bf16[528,256]{1,0:T(8,128)(2,1)S(1)} %get-tuple-element.15.refs_1_.a_high), channel_id=1, source_target_pairs={{0,3},{1,0},{2,1},{3,2},{4,7},{5,4},{6,5},{7,6},{8,11},{9,8},{10,9... | collective-permute-start | bytes 811016 | tf_op jit(solution)/shard_map/ppermute | solution.py:409
  11.4 5.6 %collective-permute-done.3.refs_5_.a_high = bf16[528,256]{1,0:T(8,128)(2,1)S(1)} collective-permute-done((bf16[528,256]{1,0:T(8,128)(2,1)S(1)}, bf16[528,256]{1,0:T(8,128)(2,1)S(1)}, u32[]{:S(2)}, u32[]{:S(2)}) %collective-permute-start.3) | collective-permute-done | bytes 270368 | tf_op jit(solution)/shard_map/ppermute | solution.py:409
  17.1 3.4 %collective-permute-start.5 = (bf16[528,256]{1,0:T(8,128)(2,1)S(1)}, bf16[528,256]{1,0:T(8,128)(2,1)S(1)}, u32[]{:S(2)}, u32[]{:S(2)}) collective-permute-start(bf16[528,256]{1,0:T(8,128)(2,1)S(1)} %collective-permute-done.3.refs_5_.a_high), channel_id=1, source_target_pairs={{0,3},{1,0},{2,1},{3,2},{4,7},{5,4},{6,5},{7,6},{8,11},{9,8},{10,9... | collective-permute-start | bytes 811016 | tf_op jit(solution)/shard_map/ppermute | solution.py:409
  20.5 5.7 %collective-permute-done.6.lo.refs_8_ = bf16[1552,256]{1,0:T(8,128)(2,1)S(1)} collective-permute-done((bf16[1552,256]{1,0:T(8,128)(2,1)S(1)}, bf16[1552,256]{1,0:T(8,128)(2,1)S(1)}, u32[]{:S(2)}, u32[]{:S(2)}) %collective-permute-start.6) | collective-permute-done | bytes 794656 | tf_op jit(solution)/shard_map/ppermute | solution.py:412
  26.2 1.0 %collective-permute-start.4 = (bf16[512,256]{1,0:T(8,128)(2,1)S(1)}, bf16[512,256]{1,0:T(8,128)(2,1)S(1)}, u32[]{:S(2)}, u32[]{:S(2)}) collective-permute-start(bf16[512,256]{1,0:T(8,128)(2,1)S(1)} %collective-permute-done.refs_2_.b_low), channel_id=1, source_target_pairs={{0,1},{1,2},{2,3},{3,0},{4,5},{5,6},{6,7},{7,4},{8,9},{9,10},{10,1... | collective-permute-start | bytes 786440 | tf_op jit(solution)/shard_map/ppermute | solution.py:409
  27.3 1.4 %collective-permute-start.8 = (bf16[512,256]{1,0:T(8,128)(2,1)S(1)}, bf16[512,256]{1,0:T(8,128)(2,1)S(1)}, u32[]{:S(2)}, u32[]{:S(2)}) collective-permute-start(bf16[512,256]{1,0:T(8,128)(2,1)S(1)} %get-tuple-element.18), channel_id=1, source_target_pairs={{0,1},{1,2},{2,3},{3,0},{4,5},{5,6},{6,7},{7,4},{8,9},{9,10},{10,1... | collective-permute-start | bytes 786440 | tf_op jit(solution)/shard_map/ppermute | solution.py:409
  28.6 1.4 %collective-permute-start.9 = (bf16[512,256]{1,0:T(8,128)(2,1)S(1)}, bf16[512,256]{1,0:T(8,128)(2,1)S(1)}, u32[]{:S(2)}, u32[]{:S(2)}) collective-permute-start(bf16[512,256]{1,0:T(8,128)(2,1)S(1)} %get-tuple-element.19), channel_id=1, source_target_pairs={{0,3},{1,0},{2,1},{3,2},{4,7},{5,4},{6,5},{7,6},{8,11},{9,8},{10,9... | collective-permute-start | bytes 786440 | tf_op jit(solution)/shard_map/ppermute | solution.py:409
  30.2 0.8 %collective-permute-done.2.refs_4_.a_low = bf16[512,256]{1,0:T(8,128)(2,1)S(1)} collective-permute-done((bf16[512,256]{1,0:T(8,128)(2,1)S(1)}, bf16[512,256]{1,0:T(8,128)(2,1)S(1)}, u32[]{:S(2)}, u32[]{:S(2)}) %collective-permute-start.2) | collective-permute-done | bytes 262176 | tf_op jit(solution)/shard_map/ppermute | solution.py:409
  31.0 4.6 %collective-permute-done.4.refs_6_.b_low = bf16[512,256]{1,0:T(8,128)(2,1)S(1)} collective-permute-done((bf16[512,256]{1,0:T(8,128)(2,1)S(1)}, bf16[512,256]{1,0:T(8,128)(2,1)S(1)}, u32[]{:S(2)}, u32[]{:S(2)}) %collective-permute-start.4) | collective-permute-done | bytes 262176 | tf_op jit(solution)/shard_map/ppermute | solution.py:409
  35.6 2.7 %collective-permute-start.11 = (bf16[1040,128]{1,0:T(8,128)(2,1)S(1)}, bf16[1040,128]{1,0:T(8,128)(2,1)S(1)}, u32[]{:S(2)}, u32[]{:S(2)}) collective-permute-start(bf16[1040,128]{1,0:T(8,128)(2,1)S(1)} %column_slices.2.own_a), channel_id=1, source_target_pairs={{4,0},{8,4},{12,8},{16,12},{20,16},{24,20},{28,24},{32,28},{36,32}... | collective-permute-start | bytes 798728 | tf_op jit(solution)/shard_map/ppermute | solution.py:412
  38.6 2.6 %collective-permute-done.8.refs_10_ = bf16[512,256]{1,0:T(8,128)(2,1)S(1)} collective-permute-done((bf16[512,256]{1,0:T(8,128)(2,1)S(1)}, bf16[512,256]{1,0:T(8,128)(2,1)S(1)}, u32[]{:S(2)}, u32[]{:S(2)}) %collective-permute-start.8) | collective-permute-done | bytes 262176 | tf_op jit(solution)/shard_map/ppermute | solution.py:409
  41.2 0.8 %collective-permute-start.13 = (bf16[1040,128]{1,0:T(8,128)(2,1)S(1)}, bf16[1040,128]{1,0:T(8,128)(2,1)S(1)}, u32[]{:S(2)}, u32[]{:S(2)}) collective-permute-start(bf16[1040,128]{1,0:T(8,128)(2,1)S(1)} %column_slices.3.own_b), channel_id=1, source_target_pairs={{4,0},{8,4},{12,8},{16,12},{20,16},{24,20},{28,24},{32,28},{36,32}... | collective-permute-start | bytes 798728 | tf_op jit(solution)/shard_map/ppermute | solution.py:412
  42.1 4.0 %near_terms.1.refs_12_ = f32[16,256,256]{2,1,0:T(8,128)S(1)} custom-call(s32[4,4]{1,0:T(4,128)S(1)} %copy-done.1, s32[4,4]{1,0:T(4,128)S(1)} %copy-done.2, bf16[512,256]{1,0:T(8,128)(2,1)S(1)} %get-tuple-element.14.refs_0_.a_low, bf16[528,256]{1,0:T(8,128)(2,1)S(1)} %get-tuple-element.15.refs_1_.a_high, ...), custom_call_target="tpu_custom_call" | custom-call | flops 2147483648 | bytes 9437184 | tf_op jit(solution)/shard_map/near_terms/pallas_call | solution.py:208
  46.1 3.8 %far_terms.1 = (bf16[16,256,256]{2,1,0:T(8,128)(2,1)S(1)}, bf16[4,256,256]{2,1,0:T(8,128)(2,1)}) custom-call(s32[4,4]{1,0:T(4,128)S(1)} %copy-done.1, bf16[512,256]{1,0:T(8,128)(2,1)S(1)} %get-tuple-element.14.refs_0_.a_low, bf16[528,256]{1,0:T(8,128)(2,1)S(1)} %get-tuple-element.15.refs_1_.a_high, bf16[512,256]{1,0:T(8,128)(2,1)S(1)} %collective-permute-done.refs_2_.b_low, ...), custom_call_target="tpu_custom_call" | custom-call | flops 805306368 | bytes 9437184 | tf_op jit(solution)/shard_map/far_terms/pallas_call | solution.py:270
  49.9 0.4 collective-permute-done.13.hi_b
  50.3 3.1 %q_product.1 = (bf16[512,128]{1,0:T(8,128)(2,1)S(1)}, bf16[512,128]{1,0:T(8,128)(2,1)S(1)}, bf16[512,128]{1,0:T(8,128)(2,1)S(1)}, bf16[512,128]{1,0:T(8,128)(2,1)S(1)}) custom-call(s32[4,4]{1,0:T(4,128)S(1)} %copy-done.1, s32[4,4]{1,0:T(4,128)S(1)} %copy-done.3, bf16[1040,128]{1,0:T(8,128)(2,1)S(1)} %collective-permute-done.10.lo_a, ...), custom_call_target="tpu_custom_call" | custom-call | flops 536870912 | bytes 5242880 | tf_op jit(solution)/shard_map/q_product/pallas_call | solution.py:348
  53.5 2.3 %collective-permute-start.15 = (bf16[512,128]{1,0:T(8,128)(2,1)S(1)}, bf16[512,128]{1,0:T(8,128)(2,1)S(1)}, u32[]{:S(2)}, u32[]{:S(2)}) collective-permute-start(bf16[512,128]{1,0:T(8,128)(2,1)S(1)} %get-tuple-element.24), channel_id=1, source_target_pairs={{0,2},{1,3},{2,0},{3,1},{4,6},{5,7},{6,4},{7,5},{8,10},{9,11},{10,... | collective-permute-start | bytes 393224 | tf_op jit(solution)/shard_map/ppermute | solution.py:409
  55.8 1.4 %collective-permute-start.16 = (bf16[512,128]{1,0:T(8,128)(2,1)S(1)}, bf16[512,128]{1,0:T(8,128)(2,1)S(1)}, u32[]{:S(2)}, u32[]{:S(2)}) collective-permute-start(bf16[512,128]{1,0:T(8,128)(2,1)S(1)} %get-tuple-element.25), channel_id=1, source_target_pairs={{0,3},{1,0},{2,1},{3,2},{4,7},{5,4},{6,5},{7,6},{8,11},{9,8},{10,9... | collective-permute-start | bytes 393224 | tf_op jit(solution)/shard_map/ppermute | solution.py:409
  57.2 3.7 %collective-permute-done.14.t1 = bf16[512,128]{1,0:T(8,128)(2,1)S(1)} collective-permute-done((bf16[512,128]{1,0:T(8,128)(2,1)S(1)}, bf16[512,128]{1,0:T(8,128)(2,1)S(1)}, u32[]{:S(2)}, u32[]{:S(2)}) %collective-permute-start.14) | collective-permute-done | bytes 131104 | tf_op jit(solution)/shard_map/ppermute | solution.py:409
  60.9 1.6 %collective-permute-done.16.t3 = bf16[512,128]{1,0:T(8,128)(2,1)S(1)} collective-permute-done((bf16[512,128]{1,0:T(8,128)(2,1)S(1)}, bf16[512,128]{1,0:T(8,128)(2,1)S(1)}, u32[]{:S(2)}, u32[]{:S(2)}) %collective-permute-start.16) | collective-permute-done | bytes 131104 | tf_op jit(solution)/shard_map/ppermute | solution.py:409
  62.5 1.1 %join.1 = bf16[4,256,256]{2,1,0:T(8,128)(2,1)} custom-call(bf16[512,128]{1,0:T(8,128)(2,1)S(1)} %get-tuple-element.22.t0, bf16[512,128]{1,0:T(8,128)(2,1)S(1)} %collective-permute-done.14.t1, bf16[512,128]{1,0:T(8,128)(2,1)S(1)} %collective-permute-done.15.t2, bf16[512,128]{1,0:T(8,128)(2,1)S(1)} %collective-permute-done.16.t3), custom_call_target="tpu_custom_call" | custom-call | tf_op jit(solution)/shard_map/join/pallas_call | solution.py:389
  (26 shorter events, 0.6 us)
Async XLA Ops:
  2.3 23.9 %collective-permute-start.6 = (bf16[1552,256]{1,0:T(8,128)(2,1)S(1)}, bf16[1552,256]{1,0:T(8,128)(2,1)S(1)}, u32[]{:S(2)}, u32[]{:S(2)}) collective-permute-start(bf16[1552,256]{1,0:T(8,128)(2,1)S(1)} %get-tuple-element.16), channel_id=1, source_target_pairs={{0,4},{4,8},{8,12},{12,16},{16,20},{20,24},{24,28},{28,32},{32,36}... | collective-permute-start | bytes 2383880 | tf_op jit(solution)/shard_map/ppermute | solution.py:412
  4.0 23.2 %collective-permute-start.7 = (bf16[1552,256]{1,0:T(8,128)(2,1)S(1)}, bf16[1552,256]{1,0:T(8,128)(2,1)S(1)}, u32[]{:S(2)}, u32[]{:S(2)}) collective-permute-start(bf16[1552,256]{1,0:T(8,128)(2,1)S(1)} %get-tuple-element.17), channel_id=1, source_target_pairs={{4,0},{8,4},{12,8},{16,12},{20,16},{24,20},{28,24},{32,28},{36,32}... | collective-permute-start | bytes 2383880 | tf_op jit(solution)/shard_map/ppermute | solution.py:412
  8.6 8.5 %collective-permute-start.3 = (bf16[528,256]{1,0:T(8,128)(2,1)S(1)}, bf16[528,256]{1,0:T(8,128)(2,1)S(1)}, u32[]{:S(2)}, u32[]{:S(2)}) collective-permute-start(bf16[528,256]{1,0:T(8,128)(2,1)S(1)} %get-tuple-element.15.refs_1_.a_high), channel_id=1, source_target_pairs={{0,3},{1,0},{2,1},{3,2},{4,7},{5,4},{6,5},{7,6},{8,11},{9,8},{10,9... | collective-permute-start | bytes 811016 | tf_op jit(solution)/shard_map/ppermute | solution.py:409
  11.3 30.7 %copy-start = (bf16[4,4,256,256]{3,2,1,0:T(8,128)(2,1)S(1)}, bf16[4,4,256,256]{3,2,1,0:T(8,128)(2,1)}, u32[]{:S(2)}) copy-start(bf16[4,4,256,256]{3,2,1,0:T(8,128)(2,1)} %param.8) | copy-start | bytes 6291460
  11.3 30.7 %copy-start.1 = (s32[4,4]{1,0:T(4,128)S(1)}, s32[4,4]{1,0:T(4,128)}, u32[]{:S(2)}) copy-start(s32[4,4]{1,0:T(4,128)} %pc.5) | copy-start | bytes 196
  11.3 30.7 %copy-start.2 = (s32[4,4]{1,0:T(4,128)S(1)}, s32[4,4]{1,0:T(4,128)}, u32[]{:S(2)}) copy-start(s32[4,4]{1,0:T(4,128)} %hc.1) | copy-start | bytes 196
  11.3 9.1 %collective-permute-start = (bf16[512,256]{1,0:T(8,128)(2,1)S(1)}, bf16[512,256]{1,0:T(8,128)(2,1)S(1)}, u32[]{:S(2)}, u32[]{:S(2)}) collective-permute-start(bf16[512,256]{1,0:T(8,128)(2,1)S(1)} %get-tuple-element.14.refs_0_.a_low), channel_id=1, source_target_pairs={{0,1},{1,2},{2,3},{3,0},{4,5},{5,6},{6,7},{7,4},{8,9},{9,10},{10,1... | collective-permute-start | bytes 786440 | tf_op jit(solution)/shard_map/ppermute | solution.py:409
  11.4 17.3 %collective-permute-start.1 = (bf16[528,256]{1,0:T(8,128)(2,1)S(1)}, bf16[528,256]{1,0:T(8,128)(2,1)S(1)}, u32[]{:S(2)}, u32[]{:S(2)}) collective-permute-start(bf16[528,256]{1,0:T(8,128)(2,1)S(1)} %get-tuple-element.15.refs_1_.a_high), channel_id=1, source_target_pairs={{0,1},{1,2},{2,3},{3,0},{4,5},{5,6},{6,7},{7,4},{8,9},{9,10},{10,1... | collective-permute-start | bytes 811016 | tf_op jit(solution)/shard_map/ppermute | solution.py:409
  17.1 21.3 %collective-permute-start.5 = (bf16[528,256]{1,0:T(8,128)(2,1)S(1)}, bf16[528,256]{1,0:T(8,128)(2,1)S(1)}, u32[]{:S(2)}, u32[]{:S(2)}) collective-permute-start(bf16[528,256]{1,0:T(8,128)(2,1)S(1)} %collective-permute-done.3.refs_5_.a_high), channel_id=1, source_target_pairs={{0,3},{1,0},{2,1},{3,2},{4,7},{5,4},{6,5},{7,6},{8,11},{9,8},{10,9... | collective-permute-start | bytes 811016 | tf_op jit(solution)/shard_map/ppermute | solution.py:409
  20.5 10.5 %collective-permute-start.2 = (bf16[512,256]{1,0:T(8,128)(2,1)S(1)}, bf16[512,256]{1,0:T(8,128)(2,1)S(1)}, u32[]{:S(2)}, u32[]{:S(2)}) collective-permute-start(bf16[512,256]{1,0:T(8,128)(2,1)S(1)} %get-tuple-element.14.refs_0_.a_low), channel_id=1, source_target_pairs={{0,3},{1,0},{2,1},{3,2},{4,7},{5,4},{6,5},{7,6},{8,11},{9,8},{10,9... | collective-permute-start | bytes 786440 | tf_op jit(solution)/shard_map/ppermute | solution.py:409
  26.2 9.4 %collective-permute-start.4 = (bf16[512,256]{1,0:T(8,128)(2,1)S(1)}, bf16[512,256]{1,0:T(8,128)(2,1)S(1)}, u32[]{:S(2)}, u32[]{:S(2)}) collective-permute-start(bf16[512,256]{1,0:T(8,128)(2,1)S(1)} %collective-permute-done.refs_2_.b_low), channel_id=1, source_target_pairs={{0,1},{1,2},{2,3},{3,0},{4,5},{5,6},{6,7},{7,4},{8,9},{9,10},{10,1... | collective-permute-start | bytes 786440 | tf_op jit(solution)/shard_map/ppermute | solution.py:409
  27.3 14.0 %collective-permute-start.8 = (bf16[512,256]{1,0:T(8,128)(2,1)S(1)}, bf16[512,256]{1,0:T(8,128)(2,1)S(1)}, u32[]{:S(2)}, u32[]{:S(2)}) collective-permute-start(bf16[512,256]{1,0:T(8,128)(2,1)S(1)} %get-tuple-element.18), channel_id=1, source_target_pairs={{0,1},{1,2},{2,3},{3,0},{4,5},{5,6},{6,7},{7,4},{8,9},{9,10},{10,1... | collective-permute-start | bytes 786440 | tf_op jit(solution)/shard_map/ppermute | solution.py:409
  28.6 17.4 %collective-permute-start.9 = (bf16[512,256]{1,0:T(8,128)(2,1)S(1)}, bf16[512,256]{1,0:T(8,128)(2,1)S(1)}, u32[]{:S(2)}, u32[]{:S(2)}) collective-permute-start(bf16[512,256]{1,0:T(8,128)(2,1)S(1)} %get-tuple-element.19), channel_id=1, source_target_pairs={{0,3},{1,0},{2,1},{3,2},{4,7},{5,4},{6,5},{7,6},{8,11},{9,8},{10,9... | collective-permute-start | bytes 786440 | tf_op jit(solution)/shard_map/ppermute | solution.py:409
  31.0 18.9 %collective-permute-start.10 = (bf16[1040,128]{1,0:T(8,128)(2,1)S(1)}, bf16[1040,128]{1,0:T(8,128)(2,1)S(1)}, u32[]{:S(2)}, u32[]{:S(2)}) collective-permute-start(bf16[1040,128]{1,0:T(8,128)(2,1)S(1)} %column_slices.2.own_a), channel_id=1, source_target_pairs={{0,4},{4,8},{8,12},{12,16},{16,20},{20,24},{24,28},{28,32},{32,36}... | collective-permute-start | bytes 798728 | tf_op jit(solution)/shard_map/ppermute | solution.py:412
  35.6 14.3 %collective-permute-start.11 = (bf16[1040,128]{1,0:T(8,128)(2,1)S(1)}, bf16[1040,128]{1,0:T(8,128)(2,1)S(1)}, u32[]{:S(2)}, u32[]{:S(2)}) collective-permute-start(bf16[1040,128]{1,0:T(8,128)(2,1)S(1)} %column_slices.2.own_a), channel_id=1, source_target_pairs={{4,0},{8,4},{12,8},{16,12},{20,16},{24,20},{28,24},{32,28},{36,32}... | collective-permute-start | bytes 798728 | tf_op jit(solution)/shard_map/ppermute | solution.py:412
  38.5 11.4 %collective-permute-start.12 = (bf16[1040,128]{1,0:T(8,128)(2,1)S(1)}, bf16[1040,128]{1,0:T(8,128)(2,1)S(1)}, u32[]{:S(2)}, u32[]{:S(2)}) collective-permute-start(bf16[1040,128]{1,0:T(8,128)(2,1)S(1)} %column_slices.3.own_b), channel_id=1, source_target_pairs={{0,4},{4,8},{8,12},{12,16},{16,20},{20,24},{24,28},{28,32},{32,36}... | collective-permute-start | bytes 798728 | tf_op jit(solution)/shard_map/ppermute | solution.py:412
  41.2 9.0 %collective-permute-start.13 = (bf16[1040,128]{1,0:T(8,128)(2,1)S(1)}, bf16[1040,128]{1,0:T(8,128)(2,1)S(1)}, u32[]{:S(2)}, u32[]{:S(2)}) collective-permute-start(bf16[1040,128]{1,0:T(8,128)(2,1)S(1)} %column_slices.3.own_b), channel_id=1, source_target_pairs={{4,0},{8,4},{12,8},{16,12},{20,16},{24,20},{28,24},{32,28},{36,32}... | collective-permute-start | bytes 798728 | tf_op jit(solution)/shard_map/ppermute | solution.py:412
  46.1 4.2 %copy-start.3 = (s32[4,4]{1,0:T(4,128)S(1)}, s32[4,4]{1,0:T(4,128)}, u32[]{:S(2)}) copy-start(s32[4,4]{1,0:T(4,128)} %qc.1) | copy-start | bytes 196
  53.4 7.5 %collective-permute-start.14 = (bf16[512,128]{1,0:T(8,128)(2,1)S(1)}, bf16[512,128]{1,0:T(8,128)(2,1)S(1)}, u32[]{:S(2)}, u32[]{:S(2)}) collective-permute-start(bf16[512,128]{1,0:T(8,128)(2,1)S(1)} %get-tuple-element.23), channel_id=1, source_target_pairs={{0,1},{1,2},{2,3},{3,0},{4,5},{5,6},{6,7},{7,4},{8,9},{9,10},{10,1... | collective-permute-start | bytes 393224 | tf_op jit(solution)/shard_map/ppermute | solution.py:409
  53.5 7.4 %collective-permute-start.15 = (bf16[512,128]{1,0:T(8,128)(2,1)S(1)}, bf16[512,128]{1,0:T(8,128)(2,1)S(1)}, u32[]{:S(2)}, u32[]{:S(2)}) collective-permute-start(bf16[512,128]{1,0:T(8,128)(2,1)S(1)} %get-tuple-element.24), channel_id=1, source_target_pairs={{0,2},{1,3},{2,0},{3,1},{4,6},{5,7},{6,4},{7,5},{8,10},{9,11},{10,... | collective-permute-start | bytes 393224 | tf_op jit(solution)/shard_map/ppermute | solution.py:409
  55.8 6.7 %collective-permute-start.16 = (bf16[512,128]{1,0:T(8,128)(2,1)S(1)}, bf16[512,128]{1,0:T(8,128)(2,1)S(1)}, u32[]{:S(2)}, u32[]{:S(2)}) collective-permute-start(bf16[512,128]{1,0:T(8,128)(2,1)S(1)} %get-tuple-element.25), channel_id=1, source_target_pairs={{0,3},{1,0},{2,1},{3,2},{4,7},{5,4},{6,5},{7,6},{8,11},{9,8},{10,9... | collective-permute-start | bytes 393224 | tf_op jit(solution)/shard_map/ppermute | solution.py:409
where the time goes:
time: 64.5 us; the launch traced here: 63.6 us
  waiting for transfers between devices  25.2 us (39%)
  starting transfers between devices  23.7 us (37%)
  Pallas kernels  13.9 us (22%)
  between operations  0.77 us (1%)
    ppermute x11, waiting for transfers between devices, turn(): lax.ppermute(x, 'depth', [(s, (s + o) % depth) for s in range(depth)])  19.1 us
    ppermute x11, starting transfers between devices, turn(): lax.ppermute(x, 'depth', [(s, (s + o) % depth) for s in range(depth)])  13.8 us
    ppermute x6, starting transfers between devices, shift(): return lax.ppermute(x, ('row', 'col'), pairs)  9.96 us
    ppermute x6, waiting for transfers between devices, shift(): return lax.ppermute(x, ('row', 'col'), pairs)  6.09 us
    pallas_call x1, Pallas kernels, near_terms(): pl.pallas_call(functools.partial(near_kernel, rows, all_rows), in_specs=[...  4 us
    pallas_call x1, Pallas kernels, far_terms(): pl.pallas_call(functools.partial(far_kernel, rows, all_rows), in_specs=[S...  3.77 us
    pallas_call x1, Pallas kernels, q_product(): pl.pallas_call(functools.partial(q_kernel, rows, all_rows), in_specs=[SME...  3.14 us
    pallas_call x1, Pallas kernels, pack(): pl.pallas_call(pack_kernel, in_specs=[HBM] * 4, out_specs=[VMEM] * 4, out...  1.65 us
  transfers between devices with their start and end apart: 17, of which 8 were waited for; matrix products, arithmetic and copies ran while one was open for 0% of the time, Pallas kernels for 13%

commit v1 on v0

--- a/solution.py
+++ b/solution.py
@@ -108,10 +108,19 @@
     )(*[hbm(a) for a in (x_columns.T, h_columns, x, h)])
 
 
-def slice_kernel(a_low, a_high, b_low, b_high, out):
+TABLE = pltpu.VMEM((16, 128), I32)
+
+
+def whole(table, parts):
+    for n, part in enumerate(parts):
+        table[8 * n : 8 * n + 8, :] = part.astype(F32).astype(I32)
+
+
+def slice_kernel(a_low, a_high, b_low, b_high, out, table):
     d = lax.axis_index("depth")
     tile = pl.ds(pl.multiple_of(d // 2 * 128, 128), 128)
     cut = a_low.shape[0]
+    whole(table, [x[x.shape[0] - PAD : x.shape[0] - PAD + 8, :128] for x in (a_high, b_high)])
     for upper in range(2):
 
         @pl.when(d % 2 == upper)
@@ -127,15 +136,16 @@
     return pl.pallas_call(
         slice_kernel,
         in_specs=[VMEM] * 4,
-        out_specs=VMEM,
-        out_shape=pltpu.VMEM((low.shape[0] + high.shape[0], 128), BF16),
+        out_specs=[VMEM, VMEM],
+        out_shape=[pltpu.VMEM((low.shape[0] + high.shape[0], 128), BF16), TABLE],
         compiler_params=pltpu.CompilerParams(vmem_limit_bytes=8 << 20),
         name="column_slices",
     )(*[vmem(x) for x in payloads])
 
 
-def first_slot_kernel(lo, hi, out_lo, out_hi):
+def first_slot_kernel(lo, hi, out_lo, out_hi, table):
     size = lo.shape[1]
+    whole(table, [x[x.shape[0] - PAD : x.shape[0] - PAD + 8, :128] for x in (lo, hi)])
     step = (lo.shape[0] - PAD) // REACH
     for source, out in ((lo, out_lo), (hi, out_hi)):
         for r in range(REACH):
@@ -147,23 +157,11 @@
     return pl.pallas_call(
         first_slot_kernel,
         in_specs=[VMEM] * 2,
-        out_specs=[VMEM] * 2,
-        out_shape=[pltpu.VMEM((REACH * size, size), BF16)] * 2,
+        out_specs=[VMEM] * 3,
+        out_shape=[pltpu.VMEM((REACH * size, size), BF16)] * 2 + [TABLE],
         compiler_params=pltpu.CompilerParams(vmem_limit_bytes=4 << 20),
         name="first_slots",
     )(vmem(lo), vmem(hi))
-
-
-def table_to_scalars(tables, tabv, tab, sem):
-    for n, table in enumerate(tables):
-        tabv[8 * n : 8 * n + 8, :] = table.astype(F32).astype(I32)
-    move = pltpu.make_async_copy(tabv, tab, sem)
-    move.start()
-    move.wait()
-
-
-def x_tables(xs):
-    return [x[x.shape[0] - PAD : x.shape[0] - PAD + 8, :128] for x in xs[1::2]]
 
 
 def x_row(xs, k, i):
@@ -186,62 +184,65 @@
     return jnp.where(found, h[pl.ds(spot, size), :], zero)
 
 
-def near_kernel(rows, all_rows, pc, hc, *refs):
-    *xs, h, total, tabv, tab, sem = refs
+def own_kernel(rows, all_rows, pc, hc, xc, low, high, h, total):
     size = h.shape[1]
     slots = pc.shape[1]
     first = lax.axis_index(("row", "col")) * rows
-    table_to_scalars(x_tables(xs), tabv, tab, sem)
     zero = jnp.zeros((size, size), BF16)
     for i in range(rows):
         for p in range(slots):
-            acc = jnp.zeros((size, size), F32)
-            for k in range(len(xs) // 2):
-                block = own_block(tab[8 * k + i, 0], first, all_rows, pc[i, p], hc, h, zero)
-                acc += jnp.dot(x_row(xs, k, i), block, preferred_element_type=F32)
+            block = own_block(xc[0, i], first, all_rows, pc[i, p], hc, h, zero)
+            total[i * slots + p] = jnp.dot(x_row((low, high), 0, i), block, preferred_element_type=F32)
+
+
+def near_kernel(rows, all_rows, pc, hc, tab_a, tab_b, *refs):
+    *xs, h, before, total = refs
+    size = h.shape[1]
+    slots = pc.shape[1]
+    first = lax.axis_index(("row", "col")) * rows
+    zero = jnp.zeros((size, size), BF16)
+    for i in range(rows):
+        for p in range(slots):
+            acc = before[i * slots + p]
+            for k in range(1, 4):
+                column = (tab_a, tab_b)[k // 2][8 * (k % 2) + i, 0]
+                block = own_block(column, first, all_rows, pc[i, p], hc, h, zero)
+                acc += jnp.dot(x_row(xs, k - 1, i), block, preferred_element_type=F32)
             total[i * slots + p] = acc
 
 
-def near_terms(pc, hc, xs, h, all_rows):
-    rows, slots = pc.shape
-    size = h.shape[-1]
-    return pl.pallas_call(
-        functools.partial(near_kernel, rows, all_rows),
-        in_specs=[SMEM] * 2 + [VMEM] * (len(xs) + 1),
+def near_terms(kernel, scalars, arrays, all_rows):
+    rows, slots = scalars[0].shape
+    size = arrays[0].shape[1]
+    terms = 3 if len(arrays) > 3 else 1
+    return pl.pallas_call(
+        functools.partial(kernel, rows, all_rows),
+        in_specs=[SMEM] * len(scalars) + [VMEM] * len(arrays),
         out_specs=VMEM,
         out_shape=pltpu.VMEM((rows * slots, size, size), F32),
-        scratch_shapes=[
-            pltpu.VMEM((4 * len(xs), 128), I32),
-            pltpu.SMEM((4 * len(xs), 128), I32),
-            pltpu.SemaphoreType.DMA,
-        ],
         cost_estimate=pl.CostEstimate(
-            flops=rows * slots * len(xs) * size**3, bytes_accessed=9 << 20, transcendentals=0
+            flops=2 * rows * slots * terms * size**3, bytes_accessed=9 << 20, transcendentals=0
         ),
         compiler_params=pltpu.CompilerParams(vmem_limit_bytes=8 << 20),
-        name="near_terms",
-    )(pc, hc, *[vmem(x) for x in xs], vmem(h.reshape(-1, size)))
-
-
-def far_kernel(rows, all_rows, pc, *refs):
-    *xs, lo, hi, lo_side, hi_side, total, full, mine, tabv, tab, sem = refs
+    )(*scalars, *[vmem(x) for x in arrays])
+
+
+def far_kernel(rows, all_rows, pc, tab_a, tab_b, tab_h, *refs):
+    *xs, lo, hi, lo_side, hi_side, total, full = refs
     size = lo.shape[1]
     slots = pc.shape[1]
-    edge = lo.shape[0] - PAD
     d, first = lax.axis_index("depth"), lax.axis_index(("row", "col")) * rows
-    table_to_scalars(
-        x_tables(xs) + [e[edge : edge + 8, :128] for e in (lo, hi)], tabv, tab, sem
-    )
     zero = jnp.zeros((size, size), BF16)
     for i in range(rows):
-        far = [(32 + r, lo, lo_side, r, 1, r - REACH) for r in range(REACH) if r - REACH >= i - REACH]
-        far += [(40 + r, hi, hi_side, r, -1, rows + r) for r in range(REACH) if rows + r <= i + REACH]
+        far = [(r, lo, lo_side, r, 1, r - REACH) for r in range(REACH) if r - REACH >= i - REACH]
+        far += [(8 + r, hi, hi_side, r, -1, rows + r) for r in range(REACH) if rows + r <= i + REACH]
         lefts = []
         for *_, j in far:
             column = lax.rem(first + j + all_rows, all_rows)
             left = zero
             for k in range(4):
-                left = jnp.where(tab[8 * k + i, 0] == column, x_row(xs, k, i), left)
+                here = (tab_a, tab_b)[k // 2][8 * (k % 2) + i, 0] == column
+                left = jnp.where(here, x_row(xs, k, i), left)
             lefts.append(left)
         for p in range(slots):
             want = pc[i, p]
@@ -249,7 +250,7 @@
             for left, (at, straight, side, r, way, _) in zip(lefts, far):
                 pick, found = jnp.int32(0), jnp.bool_(False)
                 for m in range(slots):
-                    match = tab[at, m] == want
+                    match = tab_h[at, m] == want
                     pick = jnp.where(match, m, pick)
                     found = found | match
                 n = lax.rem(way * (pick - d) + slots, slots)
@@ -261,43 +262,37 @@
                 )
                 acc += jnp.dot(left, jnp.where(found, block, zero), preferred_element_type=F32)
             full[i * slots + p] = acc.astype(BF16)
-        mine[i] = full[i * slots + d]
-
-
-def far_terms(pc, xs, edges, total, all_rows):
-    rows, slots = pc.shape
+
+
+def far_terms(scalars, xs, edges, total, all_rows):
+    rows, slots = scalars[0].shape
     size = total.shape[-1]
     return pl.pallas_call(
         functools.partial(far_kernel, rows, all_rows),
-        in_specs=[SMEM] + [VMEM] * 13,
-        out_specs=[VMEM, VMEM],
-        out_shape=[
-            pltpu.VMEM((rows * slots, size, size), BF16),
-            jax.ShapeDtypeStruct((rows, size, size), BF16),
-        ],
-        scratch_shapes=[
-            pltpu.VMEM((48, 128), I32),
-            pltpu.SMEM((48, 128), I32),
-            pltpu.SemaphoreType.DMA,
-        ],
+        in_specs=[SMEM] * 4 + [VMEM] * 13,
+        out_specs=VMEM,
+        out_shape=pltpu.VMEM((rows * slots, size, size), BF16),
         cost_estimate=pl.CostEstimate(
             flops=2 * 24 * size**3, bytes_accessed=9 << 20, transcendentals=0
         ),
         compiler_params=pltpu.CompilerParams(vmem_limit_bytes=8 << 20),
         name="far_terms",
-    )(pc, *[vmem(x) for x in (*xs, *edges, total)])
-
-
-def q_kernel(rows, all_rows, pc, qc, lo_a, own_a, hi_a, lo_b, own_b, hi_b, full, s0, s1, s2, s3, tiles, tabv, tab, res, sem):
+    )(*scalars, *[vmem(x) for x in (*xs, *edges, total)])
+
+
+def q_kernel(rows, all_rows, pc, qc, lo_a, own_a, hi_a, lo_b, own_b, hi_b, full, s0, s1, s2, s3, mine, tiles, tabv, tab, res, sem, sems):
     size = full.shape[1]
     body = rows * size
     slots = pc.shape[1]
     raw = ((lo_a, lo_b), (own_a, own_b), (hi_a, hi_b))
     d, first = lax.axis_index("depth"), lax.axis_index(("row", "col")) * rows
+    outward = copies([(full.at[i * slots + d], mine.at[i]) for i in range(rows)], sems)
+    lane = lax.broadcasted_iota(I32, (8, 128), 1) % 64 // 8
+    table = jnp.zeros((8, 128), F32)
     for n in range(3):
         for t in range(2):
-            part = raw[n][t][body : body + 8, :]
-            tabv[8 * n : 8 * n + 8, 128 * t : 128 * t + 128] = part.astype(F32).astype(I32)
+            table = jnp.where(lane == 2 * n + t, raw[n][t][body : body + 8, :].astype(F32), table)
+    tabv[...] = table.astype(I32)
     move = pltpu.make_async_copy(tabv, tab, sem)
     move.start()
     empty = 12 * slots * size
@@ -316,14 +311,14 @@
         acc = jnp.zeros((size, size), F32)
         for p in range(slots):
             j = lax.rem(pc[i, p] - first + rows + all_rows, all_rows)
-            tab_row = 8 * (j // rows) + j % rows
             picks = []
             for q in range(slots):
                 half = (q + i) % 2
                 pick = jnp.int32(empty)
                 for m in range(slots):
                     spot = (j * 4 + (m // 2) * 2 + (m % 2 != half)) * size
-                    pick = jnp.where(tab[tab_row, 64 * m] == qc[i, q], spot, pick)
+                    column = tab[j % rows, 64 * (m % 2) + 8 * (2 * (j // rows) + m // 2)]
+                    pick = jnp.where(column == qc[i, q], spot, pick)
                 picks.append(tiles[pl.ds(pl.multiple_of(pick, size), size), :])
             pairs = [(picks[0], picks[1]), (picks[2], picks[3])]
             if i % 2:
@@ -340,6 +335,8 @@
             out[e * size : e * size + size, :] = jnp.where(
                 even, res[4 * e + q // 2], res[4 * e + 2 + q // 2]
             )
+    for copy in outward:
+        copy.wait()
 
 
 def q_product(pc, qc, pieces, full, all_rows):
@@ -348,14 +345,16 @@
     return pl.pallas_call(
         functools.partial(q_kernel, rows, all_rows),
         in_specs=[SMEM] * 2 + [VMEM] * 7,
-        out_specs=[VMEM] * 4,
-        out_shape=[pltpu.VMEM((rows // 2 * size, 128), BF16)] * 4,
+        out_specs=[VMEM] * 4 + [HBM],
+        out_shape=[pltpu.VMEM((rows // 2 * size, 128), BF16)] * 4
+        + [jax.ShapeDtypeStruct((rows, size, size), BF16)],
         scratch_shapes=[
             pltpu.VMEM(((12 * slots + 1) * size, 128), BF16),
-            pltpu.VMEM((24, size), I32),
-            pltpu.SMEM((24, size), I32),
+            pltpu.VMEM((8, 128), I32),
+            pltpu.SMEM((8, 128), I32),
             pltpu.VMEM((2 * rows, size, 128), BF16),
             pltpu.SemaphoreType.DMA,
+            pltpu.SemaphoreType.DMA((rows,)),
         ],
         cost_estimate=pl.CostEstimate(
             flops=2 * rows * slots * size**3, bytes_accessed=5 << 20, transcendentals=0
@@ -418,16 +417,19 @@
     low_two, high_two = turn(low_one, 1), turn(high_three, 3)
     xs = [x_low, x_high, low_one, high_one, low_three, high_three, low_two, high_two]
 
-    a = column_slices(xs[:4])
+    h = h_blocks.reshape(-1, size)
+    tables = (p_columns, h_columns)
+    own = near_terms(own_kernel, (*tables, x_columns.T), (x_low, x_high, h), all_rows)
+    a, tab_a = column_slices(xs[:4])
     a_lo, a_hi = shift(a, up), shift(a, down)
-    send_lo, send_hi = first_slots(h_lo, h_hi)
+    send_lo, send_hi, tab_h = first_slots(h_lo, h_hi)
     edges = [h_lo, h_hi, turn(send_lo, 1), turn(send_hi, 3)]
-    b = column_slices(xs[4:])
+    b, tab_b = column_slices(xs[4:])
     b_lo, b_hi = shift(b, up), shift(b, down)
-    total = near_terms(p_columns, h_columns, xs, h_blocks, all_rows)
-    full, mine = far_terms(p_columns, xs, edges, total, all_rows)
+    total = near_terms(near_kernel, (*tables, tab_a, tab_b), (*xs[2:], h, own), all_rows)
+    full = far_terms((p_columns, tab_a, tab_b, tab_h), xs, edges, total, all_rows)
     pieces = (a_lo, a, a_hi, b_lo, b, b_hi)
-    parts = q_product(p_columns, q_columns, pieces, full, all_rows)
+    *parts, mine = q_product(p_columns, q_columns, pieces, full, all_rows)
     parts = [parts[0]] + [turn(parts[o], o) for o in range(1, depth)]
     product_q = join(parts, rows, size)
     return mine[:, None], product_q[:, None]

time: 64.5 us -> 64.4 us (level)
  waiting for transfers between devices: 25.2 us -> 26.4 us
  Pallas kernels: 13.9 us -> 12.8 us
    pallas_call x1, Pallas kernels: 3.77 us -> 2.17 us  [far_terms(): pl.pallas_call(functools.partial(far_kernel, rows, all_rows), in_specs=[S...]
    ppermute x6, waiting for transfers between devices: 6.09 us -> 7.12 us  [shift(): return lax.ppermute(x, ('row', 'col'), pairs)]
    pallas_call x3 -> x4, Pallas kernels: 4.28 us -> 4.86 us  [the longest x2 4.56 us: near_terms(): pl.pallas_call(functools.partial(kernel, rows, all_rows), in_specs=[SMEM]...]
  transfers between devices with their start and end apart: 17 -> 17, of which waited for: 8 -> 8; matrix products, arithmetic and copies ran while one was open for 0% -> 0% of each run, Pallas kernels for 13% -> 11%
where the time goes in v1:
time: 64.4 us; the launch traced here: 63.7 us
  waiting for transfers between devices  26.4 us (41%)
  starting transfers between devices  23.7 us (37%)
  Pallas kernels  12.8 us (20%)
  between operations  0.79 us (1%)
    ppermute x11, waiting for transfers between devices, turn(): lax.ppermute(x, 'depth', [(s, (s + o) % depth) for s in range(depth)])  19.2 us
    ppermute x11, starting transfers between devices, turn(): lax.ppermute(x, 'depth', [(s, (s + o) % depth) for s in range(depth)])  13.7 us
    ppermute x6, starting transfers between devices, shift(): return lax.ppermute(x, ('row', 'col'), pairs)  9.96 us
    ppermute x6, waiting for transfers between devices, shift(): return lax.ppermute(x, ('row', 'col'), pairs)  7.12 us
    pallas_call x2, Pallas kernels, near_terms(): pl.pallas_call(functools.partial(kernel, rows, all_rows), in_specs=[SMEM]...  4.56 us
    pallas_call x1, Pallas kernels, q_product(): pl.pallas_call(functools.partial(q_kernel, rows, all_rows), in_specs=[SME...  2.91 us
    pallas_call x1, Pallas kernels, far_terms(): pl.pallas_call(functools.partial(far_kernel, rows, all_rows), in_specs=[S...  2.17 us
    pallas_call x1, Pallas kernels, pack(): pl.pallas_call(pack_kernel, in_specs=[HBM] * 4, out_specs=[VMEM] * 4, out...  1.78 us
  transfers between devices with their start and end apart: 17, of which 8 were waited for; matrix products, arithmetic and copies ran while one was open for 0% of the time, Pallas kernels for 11%

profile of v1, /device:TPU:7, one launch (start us, length us, event | category | flops | bytes accessed | tf_op | source)
XLA Modules:
  0.0 63.7 jit_solution(6335437979749832393)
XLA Ops:
  0.7 1.8 %pack.1 = (bf16[512,256]{1,0:T(8,128)(2,1)S(1)}, bf16[528,256]{1,0:T(8,128)(2,1)S(1)}, bf16[1552,256]{1,0:T(8,128)(2,1)S(1)}, bf16[1552,256]{1,0:T(8,128)(2,1)S(1)}) custom-call(s32[1,4]{1,0:T(1,128)} %bitcast.12, s32[4,4]{1,0:T(4,128)} %hc.3, bf16[1024,256]{1,0:T(8,128)(2,1)} %bitcast.14, bf16[4096,256]{1,0:T(8,128)(2,1)} %bitcast.9), custom_call_target="tpu_custom_call" | custom-call | tf_op jit(solution)/shard_map/pack/pallas_call | solution.py:91
  2.5 1.7 %collective-permute-start.10 = (bf16[1552,256]{1,0:T(8,128)(2,1)S(1)}, bf16[1552,256]{1,0:T(8,128)(2,1)S(1)}, u32[]{:S(2)}, u32[]{:S(2)}) collective-permute-start(bf16[1552,256]{1,0:T(8,128)(2,1)S(1)} %get-tuple-element.24), channel_id=1, source_target_pairs={{0,4},{4,8},{8,12},{12,16},{16,20},{20,24},{24,28},{28,32},{32,36}... | collective-permute-start | bytes 2383880 | tf_op jit(solution)/shard_map/ppermute | solution.py:411
  4.2 4.6 %collective-permute-start.11 = (bf16[1552,256]{1,0:T(8,128)(2,1)S(1)}, bf16[1552,256]{1,0:T(8,128)(2,1)S(1)}, u32[]{:S(2)}, u32[]{:S(2)}) collective-permute-start(bf16[1552,256]{1,0:T(8,128)(2,1)S(1)} %get-tuple-element.25), channel_id=1, source_target_pairs={{4,0},{8,4},{12,8},{16,12},{20,16},{24,20},{28,24},{32,28},{36,32}... | collective-permute-start | bytes 2383880 | tf_op jit(solution)/shard_map/ppermute | solution.py:411
  8.8 2.7 %collective-permute-start.5 = (bf16[528,256]{1,0:T(8,128)(2,1)S(1)}, bf16[528,256]{1,0:T(8,128)(2,1)S(1)}, u32[]{:S(2)}, u32[]{:S(2)}) collective-permute-start(bf16[528,256]{1,0:T(8,128)(2,1)S(1)} %get-tuple-element.19.a_high.high.refs_1_), channel_id=1, source_target_pairs={{0,3},{1,0},{2,1},{3,2},{4,7},{5,4},{6,5},{7,6},{8,11},{9,8},{10,9... | collective-permute-start | bytes 811016 | tf_op jit(solution)/shard_map/ppermute | solution.py:408
  11.5 5.7 %collective-permute-done.5.a_high.refs_3_.refs_5_ = bf16[528,256]{1,0:T(8,128)(2,1)S(1)} collective-permute-done((bf16[528,256]{1,0:T(8,128)(2,1)S(1)}, bf16[528,256]{1,0:T(8,128)(2,1)S(1)}, u32[]{:S(2)}, u32[]{:S(2)}) %collective-permute-start.5) | collective-permute-done | bytes 270368 | tf_op jit(solution)/shard_map/ppermute | solution.py:408
  17.3 3.4 %collective-permute-start.7 = (bf16[528,256]{1,0:T(8,128)(2,1)S(1)}, bf16[528,256]{1,0:T(8,128)(2,1)S(1)}, u32[]{:S(2)}, u32[]{:S(2)}) collective-permute-start(bf16[528,256]{1,0:T(8,128)(2,1)S(1)} %collective-permute-done.5.a_high.refs_3_.refs_5_), channel_id=1, source_target_pairs={{0,3},{1,0},{2,1},{3,2},{4,7},{5,4},{6,5},{7,6},{8,11},{9,8},{10,9... | collective-permute-start | bytes 811016 | tf_op jit(solution)/shard_map/ppermute | solution.py:408
  20.7 5.7 %collective-permute-done.10.lo.refs_8_ = bf16[1552,256]{1,0:T(8,128)(2,1)S(1)} collective-permute-done((bf16[1552,256]{1,0:T(8,128)(2,1)S(1)}, bf16[1552,256]{1,0:T(8,128)(2,1)S(1)}, u32[]{:S(2)}, u32[]{:S(2)}) %collective-permute-start.10) | collective-permute-done | bytes 794656 | tf_op jit(solution)/shard_map/ppermute | solution.py:411
  26.4 1.0 %collective-permute-start.6 = (bf16[512,256]{1,0:T(8,128)(2,1)S(1)}, bf16[512,256]{1,0:T(8,128)(2,1)S(1)}, u32[]{:S(2)}, u32[]{:S(2)}) collective-permute-start(bf16[512,256]{1,0:T(8,128)(2,1)S(1)} %collective-permute-done.b_low.refs_0_.refs_2_), channel_id=1, source_target_pairs={{0,1},{1,2},{2,3},{3,0},{4,5},{5,6},{6,7},{7,4},{8,9},{9,10},{10,1... | collective-permute-start | bytes 786440 | tf_op jit(solution)/shard_map/ppermute | solution.py:408
  27.4 1.4 %collective-permute-start.12 = (bf16[512,256]{1,0:T(8,128)(2,1)S(1)}, bf16[512,256]{1,0:T(8,128)(2,1)S(1)}, u32[]{:S(2)}, u32[]{:S(2)}) collective-permute-start(bf16[512,256]{1,0:T(8,128)(2,1)S(1)} %get-tuple-element.27), channel_id=1, source_target_pairs={{0,1},{1,2},{2,3},{3,0},{4,5},{5,6},{6,7},{7,4},{8,9},{9,10},{10,1... | collective-permute-start | bytes 786440 | tf_op jit(solution)/shard_map/ppermute | solution.py:408
  28.8 1.4 %collective-permute-start.13 = (bf16[512,256]{1,0:T(8,128)(2,1)S(1)}, bf16[512,256]{1,0:T(8,128)(2,1)S(1)}, u32[]{:S(2)}, u32[]{:S(2)}) collective-permute-start(bf16[512,256]{1,0:T(8,128)(2,1)S(1)} %get-tuple-element.28), channel_id=1, source_target_pairs={{0,3},{1,0},{2,1},{3,2},{4,7},{5,4},{6,5},{7,6},{8,11},{9,8},{10,9... | collective-permute-start | bytes 786440 | tf_op jit(solution)/shard_map/ppermute | solution.py:408
  30.4 0.8 %collective-permute-done.4.a_low.refs_2_.refs_4_ = bf16[512,256]{1,0:T(8,128)(2,1)S(1)} collective-permute-done((bf16[512,256]{1,0:T(8,128)(2,1)S(1)}, bf16[512,256]{1,0:T(8,128)(2,1)S(1)}, u32[]{:S(2)}, u32[]{:S(2)}) %collective-permute-start.4) | collective-permute-done | bytes 262176 | tf_op jit(solution)/shard_map/ppermute | solution.py:408
  31.2 4.6 %collective-permute-done.6.b_low.refs_4_.refs_6_ = bf16[512,256]{1,0:T(8,128)(2,1)S(1)} collective-permute-done((bf16[512,256]{1,0:T(8,128)(2,1)S(1)}, bf16[512,256]{1,0:T(8,128)(2,1)S(1)}, u32[]{:S(2)}, u32[]{:S(2)}) %collective-permute-start.6) | collective-permute-done | bytes 262176 | tf_op jit(solution)/shard_map/ppermute | solution.py:408
  35.8 2.7 %collective-permute-start.3 = (bf16[1040,128]{1,0:T(8,128)(2,1)S(1)}, bf16[1040,128]{1,0:T(8,128)(2,1)S(1)}, u32[]{:S(2)}, u32[]{:S(2)}) collective-permute-start(bf16[1040,128]{1,0:T(8,128)(2,1)S(1)} %get-tuple-element.20.own_a), channel_id=1, source_target_pairs={{4,0},{8,4},{12,8},{16,12},{20,16},{24,20},{28,24},{32,28},{36,32}... | collective-permute-start | bytes 798728 | tf_op jit(solution)/shard_map/ppermute | solution.py:411
  38.8 2.6 %collective-permute-done.12.refs_10_ = bf16[512,256]{1,0:T(8,128)(2,1)S(1)} collective-permute-done((bf16[512,256]{1,0:T(8,128)(2,1)S(1)}, bf16[512,256]{1,0:T(8,128)(2,1)S(1)}, u32[]{:S(2)}, u32[]{:S(2)}) %collective-permute-start.12) | collective-permute-done | bytes 262176 | tf_op jit(solution)/shard_map/ppermute | solution.py:408
  41.4 0.8 %collective-permute-start.9 = (bf16[1040,128]{1,0:T(8,128)(2,1)S(1)}, bf16[1040,128]{1,0:T(8,128)(2,1)S(1)}, u32[]{:S(2)}, u32[]{:S(2)}) collective-permute-start(bf16[1040,128]{1,0:T(8,128)(2,1)S(1)} %get-tuple-element.21.own_b), channel_id=1, source_target_pairs={{4,0},{8,4},{12,8},{16,12},{20,16},{24,20},{28,24},{32,28},{36,32}... | collective-permute-start | bytes 798728 | tf_op jit(solution)/shard_map/ppermute | solution.py:411
  42.2 1.5 %shard_map.77.refs_7_ = f32[16,256,256]{2,1,0:T(8,128)S(1)} custom-call(s32[4,4]{1,0:T(4,128)S(1)} %copy-done.1, s32[4,4]{1,0:T(4,128)S(1)} %copy-done.2, s32[1,4]{1,0:T(1,128)S(1)} %bitcast.13, bf16[512,256]{1,0:T(8,128)(2,1)S(1)} %get-tuple-element.18.a_low.low.refs_0_, bf16[528,256]{1,0:T(8,128)(2,1)S(1)} %get-tuple-element.19.a_high.high.refs_1_, ...), custom_call_target="tpu_custom_call" | custom-call | flops 536870912 | bytes 9437184 | tf_op jit(solution)/shard_map/pallas_call | solution.py:218
  43.7 3.1 %shard_map.78.refs_12_ = f32[16,256,256]{2,1,0:T(8,128)S(1)} custom-call(s32[4,4]{1,0:T(4,128)S(1)} %copy-done.1, s32[4,4]{1,0:T(4,128)S(1)} %copy-done.2, s32[16,128]{1,0:T(8,128)S(1)} %get-tuple-element.22.tab_a, s32[16,128]{1,0:T(8,128)S(1)} %get-tuple-element.23.tab_b, bf16[512,256]{1,0:T(8,128)(2,1)S(1)} %collective-permute-done.b_low.refs_0_.refs_2_, ...), custom_call_target="tpu_custom_call" | custom-call | flops 1610612736 | bytes 9437184 | tf_op jit(solution)/shard_map/pallas_call | solution.py:218
  46.8 2.2 %far_terms.1.full = bf16[16,256,256]{2,1,0:T(8,128)(2,1)S(1)} custom-call(s32[4,4]{1,0:T(4,128)S(1)} %copy-done.1, s32[16,128]{1,0:T(8,128)S(1)} %get-tuple-element.22.tab_a, s32[16,128]{1,0:T(8,128)S(1)} %get-tuple-element.23.tab_b, s32[16,128]{1,0:T(8,128)S(1)} %get-tuple-element.26.tab_h, bf16[512,256]{1,0:T(8,128)(2,1)S(1)} %get-tuple-element.18.a_low.low.refs_0_, ...), custom_call_target="tpu_custom_call" | custom-call | flops 805306368 | bytes 9437184 | tf_op jit(solution)/shard_map/far_terms/pallas_call | solution.py:270
  49.0 1.4 %collective-permute-done.9.hi_b = bf16[1040,128]{1,0:T(8,128)(2,1)S(1)} collective-permute-done((bf16[1040,128]{1,0:T(8,128)(2,1)S(1)}, bf16[1040,128]{1,0:T(8,128)(2,1)S(1)}, u32[]{:S(2)}, u32[]{:S(2)}) %collective-permute-start.9) | collective-permute-done | bytes 266272 | tf_op jit(solution)/shard_map/ppermute | solution.py:411
  50.4 2.9 %q_product.1 = (bf16[512,128]{1,0:T(8,128)(2,1)S(1)}, bf16[512,128]{1,0:T(8,128)(2,1)S(1)}, bf16[512,128]{1,0:T(8,128)(2,1)S(1)}, bf16[512,128]{1,0:T(8,128)(2,1)S(1)}, bf16[4,256,256]{2,1,0:T(8,128)(2,1)}) custom-call(s32[4,4]{1,0:T(4,128)S(1)} %copy-done.1, s32[4,4]{1,0:T(4,128)S(1)} %copy-done.3, bf16[1040,128]{1,0:T(8,128)(2,1)S(1)} %collective-permute-done.2.lo_a, ...), custom_call_target="tpu_custom_call" | custom-call | flops 536870912 | bytes 5242880 | tf_op jit(solution)/shard_map/q_product/pallas_call | solution.py:345
  53.5 1.7 %collective-permute-start.15 = (bf16[512,128]{1,0:T(8,128)(2,1)S(1)}, bf16[512,128]{1,0:T(8,128)(2,1)S(1)}, u32[]{:S(2)}, u32[]{:S(2)}) collective-permute-start(bf16[512,128]{1,0:T(8,128)(2,1)S(1)} %get-tuple-element.32), channel_id=1, source_target_pairs={{0,2},{1,3},{2,0},{3,1},{4,6},{5,7},{6,4},{7,5},{8,10},{9,11},{10,... | collective-permute-start | bytes 393224 | tf_op jit(solution)/shard_map/ppermute | solution.py:408
  55.2 2.0 %collective-permute-start.16 = (bf16[512,128]{1,0:T(8,128)(2,1)S(1)}, bf16[512,128]{1,0:T(8,128)(2,1)S(1)}, u32[]{:S(2)}, u32[]{:S(2)}) collective-permute-start(bf16[512,128]{1,0:T(8,128)(2,1)S(1)} %get-tuple-element.33), channel_id=1, source_target_pairs={{0,3},{1,0},{2,1},{3,2},{4,7},{5,4},{6,5},{7,6},{8,11},{9,8},{10,9... | collective-permute-start | bytes 393224 | tf_op jit(solution)/shard_map/ppermute | solution.py:408
  57.1 5.3 %collective-permute-done.14.t1 = bf16[512,128]{1,0:T(8,128)(2,1)S(1)} collective-permute-done((bf16[512,128]{1,0:T(8,128)(2,1)S(1)}, bf16[512,128]{1,0:T(8,128)(2,1)S(1)}, u32[]{:S(2)}, u32[]{:S(2)}) %collective-permute-start.14) | collective-permute-done | bytes 131104 | tf_op jit(solution)/shard_map/ppermute | solution.py:408
  62.6 1.1 %join.1 = bf16[4,256,256]{2,1,0:T(8,128)(2,1)} custom-call(bf16[512,128]{1,0:T(8,128)(2,1)S(1)} %get-tuple-element.30.t0, bf16[512,128]{1,0:T(8,128)(2,1)S(1)} %collective-permute-done.14.t1, bf16[512,128]{1,0:T(8,128)(2,1)S(1)} %collective-permute-done.15.t2, bf16[512,128]{1,0:T(8,128)(2,1)S(1)} %collective-permute-done.16.t3), custom_call_target="tpu_custom_call" | custom-call | tf_op jit(solution)/shard_map/join/pallas_call | solution.py:388
  (29 shorter events, 0.7 us)
Async XLA Ops:
  0.6 41.6 %copy-start = (bf16[4,4,256,256]{3,2,1,0:T(8,128)(2,1)S(1)}, bf16[4,4,256,256]{3,2,1,0:T(8,128)(2,1)}, u32[]{:S(2)}) copy-start(bf16[4,4,256,256]{3,2,1,0:T(8,128)(2,1)} %param.8) | copy-start | bytes 6291460
  0.6 41.6 %copy-start.4 = (s32[4,1]{0,1:T(1,128)S(1)}, s32[4,1]{0,1:T(1,128)}, u32[]{:S(2)}) copy-start(s32[4,1]{0,1:T(1,128)} %param.7) | copy-start | bytes 52
  0.7 41.6 %copy-start.2 = (s32[4,4]{1,0:T(4,128)S(1)}, s32[4,4]{1,0:T(4,128)}, u32[]{:S(2)}) copy-start(s32[4,4]{1,0:T(4,128)} %hc.3) | copy-start | bytes 196
  0.7 41.6 %copy-start.1 = (s32[4,4]{1,0:T(4,128)S(1)}, s32[4,4]{1,0:T(4,128)}, u32[]{:S(2)}) copy-start(s32[4,4]{1,0:T(4,128)} %pc.7) | copy-start | bytes 196
  2.5 23.9 %collective-permute-start.10 = (bf16[1552,256]{1,0:T(8,128)(2,1)S(1)}, bf16[1552,256]{1,0:T(8,128)(2,1)S(1)}, u32[]{:S(2)}, u32[]{:S(2)}) collective-permute-start(bf16[1552,256]{1,0:T(8,128)(2,1)S(1)} %get-tuple-element.24), channel_id=1, source_target_pairs={{0,4},{4,8},{8,12},{12,16},{16,20},{20,24},{24,28},{28,32},{32,36}... | collective-permute-start | bytes 2383880 | tf_op jit(solution)/shard_map/ppermute | solution.py:411
  4.2 23.2 %collective-permute-start.11 = (bf16[1552,256]{1,0:T(8,128)(2,1)S(1)}, bf16[1552,256]{1,0:T(8,128)(2,1)S(1)}, u32[]{:S(2)}, u32[]{:S(2)}) collective-permute-start(bf16[1552,256]{1,0:T(8,128)(2,1)S(1)} %get-tuple-element.25), channel_id=1, source_target_pairs={{4,0},{8,4},{12,8},{16,12},{20,16},{24,20},{28,24},{32,28},{36,32}... | collective-permute-start | bytes 2383880 | tf_op jit(solution)/shard_map/ppermute | solution.py:411
  8.8 8.5 %collective-permute-start.5 = (bf16[528,256]{1,0:T(8,128)(2,1)S(1)}, bf16[528,256]{1,0:T(8,128)(2,1)S(1)}, u32[]{:S(2)}, u32[]{:S(2)}) collective-permute-start(bf16[528,256]{1,0:T(8,128)(2,1)S(1)} %get-tuple-element.19.a_high.high.refs_1_), channel_id=1, source_target_pairs={{0,3},{1,0},{2,1},{3,2},{4,7},{5,4},{6,5},{7,6},{8,11},{9,8},{10,9... | collective-permute-start | bytes 811016 | tf_op jit(solution)/shard_map/ppermute | solution.py:408
  11.5 9.2 %collective-permute-start = (bf16[512,256]{1,0:T(8,128)(2,1)S(1)}, bf16[512,256]{1,0:T(8,128)(2,1)S(1)}, u32[]{:S(2)}, u32[]{:S(2)}) collective-permute-start(bf16[512,256]{1,0:T(8,128)(2,1)S(1)} %get-tuple-element.18.a_low.low.refs_0_), channel_id=1, source_target_pairs={{0,1},{1,2},{2,3},{3,0},{4,5},{5,6},{6,7},{7,4},{8,9},{9,10},{10,1... | collective-permute-start | bytes 786440 | tf_op jit(solution)/shard_map/ppermute | solution.py:408
  11.5 17.3 %collective-permute-start.1 = (bf16[528,256]{1,0:T(8,128)(2,1)S(1)}, bf16[528,256]{1,0:T(8,128)(2,1)S(1)}, u32[]{:S(2)}, u32[]{:S(2)}) collective-permute-start(bf16[528,256]{1,0:T(8,128)(2,1)S(1)} %get-tuple-element.19.a_high.high.refs_1_), channel_id=1, source_target_pairs={{0,1},{1,2},{2,3},{3,0},{4,5},{5,6},{6,7},{7,4},{8,9},{9,10},{10,1... | collective-permute-start | bytes 811016 | tf_op jit(solution)/shard_map/ppermute | solution.py:408
  17.3 21.3 %collective-permute-start.7 = (bf16[528,256]{1,0:T(8,128)(2,1)S(1)}, bf16[528,256]{1,0:T(8,128)(2,1)S(1)}, u32[]{:S(2)}, u32[]{:S(2)}) collective-permute-start(bf16[528,256]{1,0:T(8,128)(2,1)S(1)} %collective-permute-done.5.a_high.refs_3_.refs_5_), channel_id=1, source_target_pairs={{0,3},{1,0},{2,1},{3,2},{4,7},{5,4},{6,5},{7,6},{8,11},{9,8},{10,9... | collective-permute-start | bytes 811016 | tf_op jit(solution)/shard_map/ppermute | solution.py:408
  20.7 10.5 %collective-permute-start.4 = (bf16[512,256]{1,0:T(8,128)(2,1)S(1)}, bf16[512,256]{1,0:T(8,128)(2,1)S(1)}, u32[]{:S(2)}, u32[]{:S(2)}) collective-permute-start(bf16[512,256]{1,0:T(8,128)(2,1)S(1)} %get-tuple-element.18.a_low.low.refs_0_), channel_id=1, source_target_pairs={{0,3},{1,0},{2,1},{3,2},{4,7},{5,4},{6,5},{7,6},{8,11},{9,8},{10,9... | collective-permute-start | bytes 786440 | tf_op jit(solution)/shard_map/ppermute | solution.py:408
  26.4 9.4 %collective-permute-start.6 = (bf16[512,256]{1,0:T(8,128)(2,1)S(1)}, bf16[512,256]{1,0:T(8,128)(2,1)S(1)}, u32[]{:S(2)}, u32[]{:S(2)}) collective-permute-start(bf16[512,256]{1,0:T(8,128)(2,1)S(1)} %collective-permute-done.b_low.refs_0_.refs_2_), channel_id=1, source_target_pairs={{0,1},{1,2},{2,3},{3,0},{4,5},{5,6},{6,7},{7,4},{8,9},{9,10},{10,1... | collective-permute-start | bytes 786440 | tf_op jit(solution)/shard_map/ppermute | solution.py:408
  27.4 14.0 %collective-permute-start.12 = (bf16[512,256]{1,0:T(8,128)(2,1)S(1)}, bf16[512,256]{1,0:T(8,128)(2,1)S(1)}, u32[]{:S(2)}, u32[]{:S(2)}) collective-permute-start(bf16[512,256]{1,0:T(8,128)(2,1)S(1)} %get-tuple-element.27), channel_id=1, source_target_pairs={{0,1},{1,2},{2,3},{3,0},{4,5},{5,6},{6,7},{7,4},{8,9},{9,10},{10,1... | collective-permute-start | bytes 786440 | tf_op jit(solution)/shard_map/ppermute | solution.py:408
  28.8 18.0 %collective-permute-start.13 = (bf16[512,256]{1,0:T(8,128)(2,1)S(1)}, bf16[512,256]{1,0:T(8,128)(2,1)S(1)}, u32[]{:S(2)}, u32[]{:S(2)}) collective-permute-start(bf16[512,256]{1,0:T(8,128)(2,1)S(1)} %get-tuple-element.28), channel_id=1, source_target_pairs={{0,3},{1,0},{2,1},{3,2},{4,7},{5,4},{6,5},{7,6},{8,11},{9,8},{10,9... | collective-permute-start | bytes 786440 | tf_op jit(solution)/shard_map/ppermute | solution.py:408
  31.2 17.8 %collective-permute-start.2 = (bf16[1040,128]{1,0:T(8,128)(2,1)S(1)}, bf16[1040,128]{1,0:T(8,128)(2,1)S(1)}, u32[]{:S(2)}, u32[]{:S(2)}) collective-permute-start(bf16[1040,128]{1,0:T(8,128)(2,1)S(1)} %get-tuple-element.20.own_a), channel_id=1, source_target_pairs={{0,4},{4,8},{8,12},{12,16},{16,20},{20,24},{24,28},{28,32},{32,36}... | collective-permute-start | bytes 798728 | tf_op jit(solution)/shard_map/ppermute | solution.py:411
  35.8 13.2 %collective-permute-start.3 = (bf16[1040,128]{1,0:T(8,128)(2,1)S(1)}, bf16[1040,128]{1,0:T(8,128)(2,1)S(1)}, u32[]{:S(2)}, u32[]{:S(2)}) collective-permute-start(bf16[1040,128]{1,0:T(8,128)(2,1)S(1)} %get-tuple-element.20.own_a), channel_id=1, source_target_pairs={{4,0},{8,4},{12,8},{16,12},{20,16},{24,20},{28,24},{32,28},{36,32}... | collective-permute-start | bytes 798728 | tf_op jit(solution)/shard_map/ppermute | solution.py:411
  38.7 10.3 %collective-permute-start.8 = (bf16[1040,128]{1,0:T(8,128)(2,1)S(1)}, bf16[1040,128]{1,0:T(8,128)(2,1)S(1)}, u32[]{:S(2)}, u32[]{:S(2)}) collective-permute-start(bf16[1040,128]{1,0:T(8,128)(2,1)S(1)} %get-tuple-element.21.own_b), channel_id=1, source_target_pairs={{0,4},{4,8},{8,12},{12,16},{16,20},{20,24},{24,28},{28,32},{32,36}... | collective-permute-start | bytes 798728 | tf_op jit(solution)/shard_map/ppermute | solution.py:411
  41.4 9.0 %collective-permute-start.9 = (bf16[1040,128]{1,0:T(8,128)(2,1)S(1)}, bf16[1040,128]{1,0:T(8,128)(2,1)S(1)}, u32[]{:S(2)}, u32[]{:S(2)}) collective-permute-start(bf16[1040,128]{1,0:T(8,128)(2,1)S(1)} %get-tuple-element.21.own_b), channel_id=1, source_target_pairs={{4,0},{8,4},{12,8},{16,12},{20,16},{24,20},{28,24},{32,28},{36,32}... | collective-permute-start | bytes 798728 | tf_op jit(solution)/shard_map/ppermute | solution.py:411
  46.8 3.6 %copy-start.3 = (s32[4,4]{1,0:T(4,128)S(1)}, s32[4,4]{1,0:T(4,128)}, u32[]{:S(2)}) copy-start(s32[4,4]{1,0:T(4,128)} %qc.1) | copy-start | bytes 196
  53.4 9.1 %collective-permute-start.14 = (bf16[512,128]{1,0:T(8,128)(2,1)S(1)}, bf16[512,128]{1,0:T(8,128)(2,1)S(1)}, u32[]{:S(2)}, u32[]{:S(2)}) collective-permute-start(bf16[512,128]{1,0:T(8,128)(2,1)S(1)} %get-tuple-element.31), channel_id=1, source_target_pairs={{0,1},{1,2},{2,3},{3,0},{4,5},{5,6},{6,7},{7,4},{8,9},{9,10},{10,1... | collective-permute-start | bytes 393224 | tf_op jit(solution)/shard_map/ppermute | solution.py:408
  53.5 9.0 %collective-permute-start.15 = (bf16[512,128]{1,0:T(8,128)(2,1)S(1)}, bf16[512,128]{1,0:T(8,128)(2,1)S(1)}, u32[]{:S(2)}, u32[]{:S(2)}) collective-permute-start(bf16[512,128]{1,0:T(8,128)(2,1)S(1)} %get-tuple-element.32), channel_id=1, source_target_pairs={{0,2},{1,3},{2,0},{3,1},{4,6},{5,7},{6,4},{7,5},{8,10},{9,11},{10,... | collective-permute-start | bytes 393224 | tf_op jit(solution)/shard_map/ppermute | solution.py:408
  55.2 7.4 %collective-permute-start.16 = (bf16[512,128]{1,0:T(8,128)(2,1)S(1)}, bf16[512,128]{1,0:T(8,128)(2,1)S(1)}, u32[]{:S(2)}, u32[]{:S(2)}) collective-permute-start(bf16[512,128]{1,0:T(8,128)(2,1)S(1)} %get-tuple-element.33), channel_id=1, source_target_pairs={{0,3},{1,0},{2,1},{3,2},{4,7},{5,4},{6,5},{7,6},{8,11},{9,8},{10,9... | collective-permute-start | bytes 393224 | tf_op jit(solution)/shard_map/ppermute | solution.py:408

commit v2 on v1

--- a/solution.py
+++ b/solution.py
@@ -364,7 +364,7 @@
     )(pc, qc, *[vmem(x) for x in (*pieces, full)])
 
 
-def join_kernel(t0, t1, t2, t3, out, held):
+def join_kernel(t0, t1, t2, t3, out, held, ready, sems):
     size, d = out.shape[1], lax.axis_index("depth")
     for o, t in enumerate((t0, t1, t2, t3)):
         held[lax.rem(d - o + 4, 4)] = t[...]
@@ -381,16 +381,23 @@
                         b = swapped(b)
                     else:
                         a = swapped(a)
-                    out[i, :, 128 * t : 128 * t + 128] = jnp.where(mask, a, b)
+                    ready[i, :, 128 * t : 128 * t + 128] = jnp.where(mask, a, b)
+                pltpu.make_async_copy(ready.at[i], out.at[i], sems.at[i]).start()
+    for i in range(out.shape[0]):
+        pltpu.make_async_copy(ready.at[i], out.at[i], sems.at[i]).wait()
 
 
 def join(parts, rows, size):
     return pl.pallas_call(
         join_kernel,
         in_specs=[VMEM] * 4,
-        out_specs=VMEM,
+        out_specs=HBM,
         out_shape=jax.ShapeDtypeStruct((rows, size, size), BF16),
-        scratch_shapes=[pltpu.VMEM((4, *parts[0].shape), BF16)],
+        scratch_shapes=[
+            pltpu.VMEM((4, *parts[0].shape), BF16),
+            pltpu.VMEM((rows, size, size), BF16),
+            pltpu.SemaphoreType.DMA((rows,)),
+        ],
         compiler_params=pltpu.CompilerParams(vmem_limit_bytes=8 << 20),
         name="join",
     )(*[vmem(x) for x in parts])

time: 64.4 us -> 64.5 us (level)
  no operation moved by 1% of the time
where the time goes in v2:
time: 64.5 us; the launch traced here: 63.7 us
  waiting for transfers between devices  26.4 us (41%)
  starting transfers between devices  23.7 us (37%)
  Pallas kernels  12.7 us (20%)
  between operations  0.95 us (1%)
    ppermute x11, waiting for transfers between devices, turn(): lax.ppermute(x, 'depth', [(s, (s + o) % depth) for s in range(depth)])  19.2 us
    ppermute x11, starting transfers between devices, turn(): lax.ppermute(x, 'depth', [(s, (s + o) % depth) for s in range(depth)])  13.7 us
    ppermute x6, starting transfers between devices, shift(): return lax.ppermute(x, ('row', 'col'), pairs)  9.96 us
    ppermute x6, waiting for transfers between devices, shift(): return lax.ppermute(x, ('row', 'col'), pairs)  7.12 us
    pallas_call x2, Pallas kernels, near_terms(): pl.pallas_call(functools.partial(kernel, rows, all_rows), in_specs=[SMEM]...  4.56 us
    pallas_call x1, Pallas kernels, q_product(): pl.pallas_call(functools.partial(q_kernel, rows, all_rows), in_specs=[SME...  2.91 us
    pallas_call x1, Pallas kernels, far_terms(): pl.pallas_call(functools.partial(far_kernel, rows, all_rows), in_specs=[S...  2.17 us
    pallas_call x1, Pallas kernels, pack(): pl.pallas_call(pack_kernel, in_specs=[HBM] * 4, out_specs=[VMEM] * 4, out...  1.78 us
  transfers between devices with their start and end apart: 17, of which 8 were waited for; matrix products, arithmetic and copies ran while one was open for 0% of the time, Pallas kernels for 11%

profile of v2, /device:TPU:7, one launch (start us, length us, event | category | flops | bytes accessed | tf_op | source)
XLA Modules:
  0.0 63.7 jit_solution(9920825161922632005)
XLA Ops:
  0.7 1.8 %pack.1 = (bf16[512,256]{1,0:T(8,128)(2,1)S(1)}, bf16[528,256]{1,0:T(8,128)(2,1)S(1)}, bf16[1552,256]{1,0:T(8,128)(2,1)S(1)}, bf16[1552,256]{1,0:T(8,128)(2,1)S(1)}) custom-call(s32[1,4]{1,0:T(1,128)} %bitcast.12, s32[4,4]{1,0:T(4,128)} %hc.3, bf16[1024,256]{1,0:T(8,128)(2,1)} %bitcast.14, bf16[4096,256]{1,0:T(8,128)(2,1)} %bitcast.9), custom_call_target="tpu_custom_call" | custom-call | tf_op jit(solution)/shard_map/pack/pallas_call | solution.py:91
  2.5 1.7 %collective-permute-start.10 = (bf16[1552,256]{1,0:T(8,128)(2,1)S(1)}, bf16[1552,256]{1,0:T(8,128)(2,1)S(1)}, u32[]{:S(2)}, u32[]{:S(2)}) collective-permute-start(bf16[1552,256]{1,0:T(8,128)(2,1)S(1)} %get-tuple-element.24), channel_id=1, source_target_pairs={{0,4},{4,8},{8,12},{12,16},{16,20},{20,24},{24,28},{28,32},{32,36}... | collective-permute-start | bytes 2383880 | tf_op jit(solution)/shard_map/ppermute | solution.py:418
  4.2 4.6 %collective-permute-start.11 = (bf16[1552,256]{1,0:T(8,128)(2,1)S(1)}, bf16[1552,256]{1,0:T(8,128)(2,1)S(1)}, u32[]{:S(2)}, u32[]{:S(2)}) collective-permute-start(bf16[1552,256]{1,0:T(8,128)(2,1)S(1)} %get-tuple-element.25), channel_id=1, source_target_pairs={{4,0},{8,4},{12,8},{16,12},{20,16},{24,20},{28,24},{32,28},{36,32}... | collective-permute-start | bytes 2383880 | tf_op jit(solution)/shard_map/ppermute | solution.py:418
  8.8 2.7 %collective-permute-start.5 = (bf16[528,256]{1,0:T(8,128)(2,1)S(1)}, bf16[528,256]{1,0:T(8,128)(2,1)S(1)}, u32[]{:S(2)}, u32[]{:S(2)}) collective-permute-start(bf16[528,256]{1,0:T(8,128)(2,1)S(1)} %get-tuple-element.19.a_high.high.refs_1_), channel_id=1, source_target_pairs={{0,3},{1,0},{2,1},{3,2},{4,7},{5,4},{6,5},{7,6},{8,11},{9,8},{10,9... | collective-permute-start | bytes 811016 | tf_op jit(solution)/shard_map/ppermute | solution.py:415
  11.5 5.7 %collective-permute-done.5.a_high.refs_3_.refs_5_ = bf16[528,256]{1,0:T(8,128)(2,1)S(1)} collective-permute-done((bf16[528,256]{1,0:T(8,128)(2,1)S(1)}, bf16[528,256]{1,0:T(8,128)(2,1)S(1)}, u32[]{:S(2)}, u32[]{:S(2)}) %collective-permute-start.5) | collective-permute-done | bytes 270368 | tf_op jit(solution)/shard_map/ppermute | solution.py:415
  17.3 3.4 %collective-permute-start.7 = (bf16[528,256]{1,0:T(8,128)(2,1)S(1)}, bf16[528,256]{1,0:T(8,128)(2,1)S(1)}, u32[]{:S(2)}, u32[]{:S(2)}) collective-permute-start(bf16[528,256]{1,0:T(8,128)(2,1)S(1)} %collective-permute-done.5.a_high.refs_3_.refs_5_), channel_id=1, source_target_pairs={{0,3},{1,0},{2,1},{3,2},{4,7},{5,4},{6,5},{7,6},{8,11},{9,8},{10,9... | collective-permute-start | bytes 811016 | tf_op jit(solution)/shard_map/ppermute | solution.py:415
  20.7 5.7 %collective-permute-done.10.lo.refs_8_ = bf16[1552,256]{1,0:T(8,128)(2,1)S(1)} collective-permute-done((bf16[1552,256]{1,0:T(8,128)(2,1)S(1)}, bf16[1552,256]{1,0:T(8,128)(2,1)S(1)}, u32[]{:S(2)}, u32[]{:S(2)}) %collective-permute-start.10) | collective-permute-done | bytes 794656 | tf_op jit(solution)/shard_map/ppermute | solution.py:418
  26.4 1.0 %collective-permute-start.6 = (bf16[512,256]{1,0:T(8,128)(2,1)S(1)}, bf16[512,256]{1,0:T(8,128)(2,1)S(1)}, u32[]{:S(2)}, u32[]{:S(2)}) collective-permute-start(bf16[512,256]{1,0:T(8,128)(2,1)S(1)} %collective-permute-done.b_low.refs_0_.refs_2_), channel_id=1, source_target_pairs={{0,1},{1,2},{2,3},{3,0},{4,5},{5,6},{6,7},{7,4},{8,9},{9,10},{10,1... | collective-permute-start | bytes 786440 | tf_op jit(solution)/shard_map/ppermute | solution.py:415
  27.4 1.4 %collective-permute-start.12 = (bf16[512,256]{1,0:T(8,128)(2,1)S(1)}, bf16[512,256]{1,0:T(8,128)(2,1)S(1)}, u32[]{:S(2)}, u32[]{:S(2)}) collective-permute-start(bf16[512,256]{1,0:T(8,128)(2,1)S(1)} %get-tuple-element.27), channel_id=1, source_target_pairs={{0,1},{1,2},{2,3},{3,0},{4,5},{5,6},{6,7},{7,4},{8,9},{9,10},{10,1... | collective-permute-start | bytes 786440 | tf_op jit(solution)/shard_map/ppermute | solution.py:415
  28.8 1.4 %collective-permute-start.13 = (bf16[512,256]{1,0:T(8,128)(2,1)S(1)}, bf16[512,256]{1,0:T(8,128)(2,1)S(1)}, u32[]{:S(2)}, u32[]{:S(2)}) collective-permute-start(bf16[512,256]{1,0:T(8,128)(2,1)S(1)} %get-tuple-element.28), channel_id=1, source_target_pairs={{0,3},{1,0},{2,1},{3,2},{4,7},{5,4},{6,5},{7,6},{8,11},{9,8},{10,9... | collective-permute-start | bytes 786440 | tf_op jit(solution)/shard_map/ppermute | solution.py:415
  30.4 0.8 %collective-permute-done.4.a_low.refs_2_.refs_4_ = bf16[512,256]{1,0:T(8,128)(2,1)S(1)} collective-permute-done((bf16[512,256]{1,0:T(8,128)(2,1)S(1)}, bf16[512,256]{1,0:T(8,128)(2,1)S(1)}, u32[]{:S(2)}, u32[]{:S(2)}) %collective-permute-start.4) | collective-permute-done | bytes 262176 | tf_op jit(solution)/shard_map/ppermute | solution.py:415
  31.2 4.6 %collective-permute-done.6.b_low.refs_4_.refs_6_ = bf16[512,256]{1,0:T(8,128)(2,1)S(1)} collective-permute-done((bf16[512,256]{1,0:T(8,128)(2,1)S(1)}, bf16[512,256]{1,0:T(8,128)(2,1)S(1)}, u32[]{:S(2)}, u32[]{:S(2)}) %collective-permute-start.6) | collective-permute-done | bytes 262176 | tf_op jit(solution)/shard_map/ppermute | solution.py:415
  35.8 2.7 %collective-permute-start.3 = (bf16[1040,128]{1,0:T(8,128)(2,1)S(1)}, bf16[1040,128]{1,0:T(8,128)(2,1)S(1)}, u32[]{:S(2)}, u32[]{:S(2)}) collective-permute-start(bf16[1040,128]{1,0:T(8,128)(2,1)S(1)} %get-tuple-element.20.own_a), channel_id=1, source_target_pairs={{4,0},{8,4},{12,8},{16,12},{20,16},{24,20},{28,24},{32,28},{36,32}... | collective-permute-start | bytes 798728 | tf_op jit(solution)/shard_map/ppermute | solution.py:418
  38.8 2.6 %collective-permute-done.12.refs_10_ = bf16[512,256]{1,0:T(8,128)(2,1)S(1)} collective-permute-done((bf16[512,256]{1,0:T(8,128)(2,1)S(1)}, bf16[512,256]{1,0:T(8,128)(2,1)S(1)}, u32[]{:S(2)}, u32[]{:S(2)}) %collective-permute-start.12) | collective-permute-done | bytes 262176 | tf_op jit(solution)/shard_map/ppermute | solution.py:415
  41.4 0.8 %collective-permute-start.9 = (bf16[1040,128]{1,0:T(8,128)(2,1)S(1)}, bf16[1040,128]{1,0:T(8,128)(2,1)S(1)}, u32[]{:S(2)}, u32[]{:S(2)}) collective-permute-start(bf16[1040,128]{1,0:T(8,128)(2,1)S(1)} %get-tuple-element.21.own_b), channel_id=1, source_target_pairs={{4,0},{8,4},{12,8},{16,12},{20,16},{24,20},{28,24},{32,28},{36,32}... | collective-permute-start | bytes 798728 | tf_op jit(solution)/shard_map/ppermute | solution.py:418
  42.2 1.5 %shard_map.77.refs_7_ = f32[16,256,256]{2,1,0:T(8,128)S(1)} custom-call(s32[4,4]{1,0:T(4,128)S(1)} %copy-done.1, s32[4,4]{1,0:T(4,128)S(1)} %copy-done.2, s32[1,4]{1,0:T(1,128)S(1)} %bitcast.13, bf16[512,256]{1,0:T(8,128)(2,1)S(1)} %get-tuple-element.18.a_low.low.refs_0_, bf16[528,256]{1,0:T(8,128)(2,1)S(1)} %get-tuple-element.19.a_high.high.refs_1_, ...), custom_call_target="tpu_custom_call" | custom-call | flops 536870912 | bytes 9437184 | tf_op jit(solution)/shard_map/pallas_call | solution.py:218
  43.7 3.1 %shard_map.78.refs_12_ = f32[16,256,256]{2,1,0:T(8,128)S(1)} custom-call(s32[4,4]{1,0:T(4,128)S(1)} %copy-done.1, s32[4,4]{1,0:T(4,128)S(1)} %copy-done.2, s32[16,128]{1,0:T(8,128)S(1)} %get-tuple-element.22.tab_a, s32[16,128]{1,0:T(8,128)S(1)} %get-tuple-element.23.tab_b, bf16[512,256]{1,0:T(8,128)(2,1)S(1)} %collective-permute-done.b_low.refs_0_.refs_2_, ...), custom_call_target="tpu_custom_call" | custom-call | flops 1610612736 | bytes 9437184 | tf_op jit(solution)/shard_map/pallas_call | solution.py:218
  46.8 2.2 %far_terms.1.full = bf16[16,256,256]{2,1,0:T(8,128)(2,1)S(1)} custom-call(s32[4,4]{1,0:T(4,128)S(1)} %copy-done.1, s32[16,128]{1,0:T(8,128)S(1)} %get-tuple-element.22.tab_a, s32[16,128]{1,0:T(8,128)S(1)} %get-tuple-element.23.tab_b, s32[16,128]{1,0:T(8,128)S(1)} %get-tuple-element.26.tab_h, bf16[512,256]{1,0:T(8,128)(2,1)S(1)} %get-tuple-element.18.a_low.low.refs_0_, ...), custom_call_target="tpu_custom_call" | custom-call | flops 805306368 | bytes 9437184 | tf_op jit(solution)/shard_map/far_terms/pallas_call | solution.py:270
  49.0 1.4 %collective-permute-done.9.hi_b = bf16[1040,128]{1,0:T(8,128)(2,1)S(1)} collective-permute-done((bf16[1040,128]{1,0:T(8,128)(2,1)S(1)}, bf16[1040,128]{1,0:T(8,128)(2,1)S(1)}, u32[]{:S(2)}, u32[]{:S(2)}) %collective-permute-start.9) | collective-permute-done | bytes 266272 | tf_op jit(solution)/shard_map/ppermute | solution.py:418
  50.4 2.9 %q_product.1 = (bf16[512,128]{1,0:T(8,128)(2,1)S(1)}, bf16[512,128]{1,0:T(8,128)(2,1)S(1)}, bf16[512,128]{1,0:T(8,128)(2,1)S(1)}, bf16[512,128]{1,0:T(8,128)(2,1)S(1)}, bf16[4,256,256]{2,1,0:T(8,128)(2,1)}) custom-call(s32[4,4]{1,0:T(4,128)S(1)} %copy-done.1, s32[4,4]{1,0:T(4,128)S(1)} %copy-done.3, bf16[1040,128]{1,0:T(8,128)(2,1)S(1)} %collective-permute-done.2.lo_a, ...), custom_call_target="tpu_custom_call" | custom-call | flops 536870912 | bytes 5242880 | tf_op jit(solution)/shard_map/q_product/pallas_call | solution.py:345
  53.5 1.7 %collective-permute-start.15 = (bf16[512,128]{1,0:T(8,128)(2,1)S(1)}, bf16[512,128]{1,0:T(8,128)(2,1)S(1)}, u32[]{:S(2)}, u32[]{:S(2)}) collective-permute-start(bf16[512,128]{1,0:T(8,128)(2,1)S(1)} %get-tuple-element.32), channel_id=1, source_target_pairs={{0,2},{1,3},{2,0},{3,1},{4,6},{5,7},{6,4},{7,5},{8,10},{9,11},{10,... | collective-permute-start | bytes 393224 | tf_op jit(solution)/shard_map/ppermute | solution.py:415
  55.2 2.0 %collective-permute-start.16 = (bf16[512,128]{1,0:T(8,128)(2,1)S(1)}, bf16[512,128]{1,0:T(8,128)(2,1)S(1)}, u32[]{:S(2)}, u32[]{:S(2)}) collective-permute-start(bf16[512,128]{1,0:T(8,128)(2,1)S(1)} %get-tuple-element.33), channel_id=1, source_target_pairs={{0,3},{1,0},{2,1},{3,2},{4,7},{5,4},{6,5},{7,6},{8,11},{9,8},{10,9... | collective-permute-start | bytes 393224 | tf_op jit(solution)/shard_map/ppermute | solution.py:415
  57.1 5.3 %collective-permute-done.14.t1 = bf16[512,128]{1,0:T(8,128)(2,1)S(1)} collective-permute-done((bf16[512,128]{1,0:T(8,128)(2,1)S(1)}, bf16[512,128]{1,0:T(8,128)(2,1)S(1)}, u32[]{:S(2)}, u32[]{:S(2)}) %collective-permute-start.14) | collective-permute-done | bytes 131104 | tf_op jit(solution)/shard_map/ppermute | solution.py:415
  62.6 1.0 %join.1 = bf16[4,256,256]{2,1,0:T(8,128)(2,1)} custom-call(bf16[512,128]{1,0:T(8,128)(2,1)S(1)} %get-tuple-element.30.t0, bf16[512,128]{1,0:T(8,128)(2,1)S(1)} %collective-permute-done.14.t1, bf16[512,128]{1,0:T(8,128)(2,1)S(1)} %collective-permute-done.15.t2, bf16[512,128]{1,0:T(8,128)(2,1)S(1)} %collective-permute-done.16.t3), custom_call_target="tpu_custom_call" | custom-call | tf_op jit(solution)/shard_map/join/pallas_call | solution.py:391
  (29 shorter events, 0.7 us)
Async XLA Ops:
  0.6 41.6 %copy-start = (bf16[4,4,256,256]{3,2,1,0:T(8,128)(2,1)S(1)}, bf16[4,4,256,256]{3,2,1,0:T(8,128)(2,1)}, u32[]{:S(2)}) copy-start(bf16[4,4,256,256]{3,2,1,0:T(8,128)(2,1)} %param.8) | copy-start | bytes 6291460
  0.6 41.6 %copy-start.4 = (s32[4,1]{0,1:T(1,128)S(1)}, s32[4,1]{0,1:T(1,128)}, u32[]{:S(2)}) copy-start(s32[4,1]{0,1:T(1,128)} %param.7) | copy-start | bytes 52
  0.7 41.6 %copy-start.2 = (s32[4,4]{1,0:T(4,128)S(1)}, s32[4,4]{1,0:T(4,128)}, u32[]{:S(2)}) copy-start(s32[4,4]{1,0:T(4,128)} %hc.3) | copy-start | bytes 196
  0.7 41.6 %copy-start.1 = (s32[4,4]{1,0:T(4,128)S(1)}, s32[4,4]{1,0:T(4,128)}, u32[]{:S(2)}) copy-start(s32[4,4]{1,0:T(4,128)} %pc.7) | copy-start | bytes 196
  2.5 23.9 %collective-permute-start.10 = (bf16[1552,256]{1,0:T(8,128)(2,1)S(1)}, bf16[1552,256]{1,0:T(8,128)(2,1)S(1)}, u32[]{:S(2)}, u32[]{:S(2)}) collective-permute-start(bf16[1552,256]{1,0:T(8,128)(2,1)S(1)} %get-tuple-element.24), channel_id=1, source_target_pairs={{0,4},{4,8},{8,12},{12,16},{16,20},{20,24},{24,28},{28,32},{32,36}... | collective-permute-start | bytes 2383880 | tf_op jit(solution)/shard_map/ppermute | solution.py:418
  4.2 23.2 %collective-permute-start.11 = (bf16[1552,256]{1,0:T(8,128)(2,1)S(1)}, bf16[1552,256]{1,0:T(8,128)(2,1)S(1)}, u32[]{:S(2)}, u32[]{:S(2)}) collective-permute-start(bf16[1552,256]{1,0:T(8,128)(2,1)S(1)} %get-tuple-element.25), channel_id=1, source_target_pairs={{4,0},{8,4},{12,8},{16,12},{20,16},{24,20},{28,24},{32,28},{36,32}... | collective-permute-start | bytes 2383880 | tf_op jit(solution)/shard_map/ppermute | solution.py:418
  8.8 8.5 %collective-permute-start.5 = (bf16[528,256]{1,0:T(8,128)(2,1)S(1)}, bf16[528,256]{1,0:T(8,128)(2,1)S(1)}, u32[]{:S(2)}, u32[]{:S(2)}) collective-permute-start(bf16[528,256]{1,0:T(8,128)(2,1)S(1)} %get-tuple-element.19.a_high.high.refs_1_), channel_id=1, source_target_pairs={{0,3},{1,0},{2,1},{3,2},{4,7},{5,4},{6,5},{7,6},{8,11},{9,8},{10,9... | collective-permute-start | bytes 811016 | tf_op jit(solution)/shard_map/ppermute | solution.py:415
  11.5 9.2 %collective-permute-start = (bf16[512,256]{1,0:T(8,128)(2,1)S(1)}, bf16[512,256]{1,0:T(8,128)(2,1)S(1)}, u32[]{:S(2)}, u32[]{:S(2)}) collective-permute-start(bf16[512,256]{1,0:T(8,128)(2,1)S(1)} %get-tuple-element.18.a_low.low.refs_0_), channel_id=1, source_target_pairs={{0,1},{1,2},{2,3},{3,0},{4,5},{5,6},{6,7},{7,4},{8,9},{9,10},{10,1... | collective-permute-start | bytes 786440 | tf_op jit(solution)/shard_map/ppermute | solution.py:415
  11.5 17.3 %collective-permute-start.1 = (bf16[528,256]{1,0:T(8,128)(2,1)S(1)}, bf16[528,256]{1,0:T(8,128)(2,1)S(1)}, u32[]{:S(2)}, u32[]{:S(2)}) collective-permute-start(bf16[528,256]{1,0:T(8,128)(2,1)S(1)} %get-tuple-element.19.a_high.high.refs_1_), channel_id=1, source_target_pairs={{0,1},{1,2},{2,3},{3,0},{4,5},{5,6},{6,7},{7,4},{8,9},{9,10},{10,1... | collective-permute-start | bytes 811016 | tf_op jit(solution)/shard_map/ppermute | solution.py:415
  17.3 21.3 %collective-permute-start.7 = (bf16[528,256]{1,0:T(8,128)(2,1)S(1)}, bf16[528,256]{1,0:T(8,128)(2,1)S(1)}, u32[]{:S(2)}, u32[]{:S(2)}) collective-permute-start(bf16[528,256]{1,0:T(8,128)(2,1)S(1)} %collective-permute-done.5.a_high.refs_3_.refs_5_), channel_id=1, source_target_pairs={{0,3},{1,0},{2,1},{3,2},{4,7},{5,4},{6,5},{7,6},{8,11},{9,8},{10,9... | collective-permute-start | bytes 811016 | tf_op jit(solution)/shard_map/ppermute | solution.py:415
  20.7 10.5 %collective-permute-start.4 = (bf16[512,256]{1,0:T(8,128)(2,1)S(1)}, bf16[512,256]{1,0:T(8,128)(2,1)S(1)}, u32[]{:S(2)}, u32[]{:S(2)}) collective-permute-start(bf16[512,256]{1,0:T(8,128)(2,1)S(1)} %get-tuple-element.18.a_low.low.refs_0_), channel_id=1, source_target_pairs={{0,3},{1,0},{2,1},{3,2},{4,7},{5,4},{6,5},{7,6},{8,11},{9,8},{10,9... | collective-permute-start | bytes 786440 | tf_op jit(solution)/shard_map/ppermute | solution.py:415
  26.4 9.4 %collective-permute-start.6 = (bf16[512,256]{1,0:T(8,128)(2,1)S(1)}, bf16[512,256]{1,0:T(8,128)(2,1)S(1)}, u32[]{:S(2)}, u32[]{:S(2)}) collective-permute-start(bf16[512,256]{1,0:T(8,128)(2,1)S(1)} %collective-permute-done.b_low.refs_0_.refs_2_), channel_id=1, source_target_pairs={{0,1},{1,2},{2,3},{3,0},{4,5},{5,6},{6,7},{7,4},{8,9},{9,10},{10,1... | collective-permute-start | bytes 786440 | tf_op jit(solution)/shard_map/ppermute | solution.py:415
  27.4 14.0 %collective-permute-start.12 = (bf16[512,256]{1,0:T(8,128)(2,1)S(1)}, bf16[512,256]{1,0:T(8,128)(2,1)S(1)}, u32[]{:S(2)}, u32[]{:S(2)}) collective-permute-start(bf16[512,256]{1,0:T(8,128)(2,1)S(1)} %get-tuple-element.27), channel_id=1, source_target_pairs={{0,1},{1,2},{2,3},{3,0},{4,5},{5,6},{6,7},{7,4},{8,9},{9,10},{10,1... | collective-permute-start | bytes 786440 | tf_op jit(solution)/shard_map/ppermute | solution.py:415
  28.8 18.0 %collective-permute-start.13 = (bf16[512,256]{1,0:T(8,128)(2,1)S(1)}, bf16[512,256]{1,0:T(8,128)(2,1)S(1)}, u32[]{:S(2)}, u32[]{:S(2)}) collective-permute-start(bf16[512,256]{1,0:T(8,128)(2,1)S(1)} %get-tuple-element.28), channel_id=1, source_target_pairs={{0,3},{1,0},{2,1},{3,2},{4,7},{5,4},{6,5},{7,6},{8,11},{9,8},{10,9... | collective-permute-start | bytes 786440 | tf_op jit(solution)/shard_map/ppermute | solution.py:415
  31.2 17.8 %collective-permute-start.2 = (bf16[1040,128]{1,0:T(8,128)(2,1)S(1)}, bf16[1040,128]{1,0:T(8,128)(2,1)S(1)}, u32[]{:S(2)}, u32[]{:S(2)}) collective-permute-start(bf16[1040,128]{1,0:T(8,128)(2,1)S(1)} %get-tuple-element.20.own_a), channel_id=1, source_target_pairs={{0,4},{4,8},{8,12},{12,16},{16,20},{20,24},{24,28},{28,32},{32,36}... | collective-permute-start | bytes 798728 | tf_op jit(solution)/shard_map/ppermute | solution.py:418
  35.8 13.2 %collective-permute-start.3 = (bf16[1040,128]{1,0:T(8,128)(2,1)S(1)}, bf16[1040,128]{1,0:T(8,128)(2,1)S(1)}, u32[]{:S(2)}, u32[]{:S(2)}) collective-permute-start(bf16[1040,128]{1,0:T(8,128)(2,1)S(1)} %get-tuple-element.20.own_a), channel_id=1, source_target_pairs={{4,0},{8,4},{12,8},{16,12},{20,16},{24,20},{28,24},{32,28},{36,32}... | collective-permute-start | bytes 798728 | tf_op jit(solution)/shard_map/ppermute | solution.py:418
  38.7 10.3 %collective-permute-start.8 = (bf16[1040,128]{1,0:T(8,128)(2,1)S(1)}, bf16[1040,128]{1,0:T(8,128)(2,1)S(1)}, u32[]{:S(2)}, u32[]{:S(2)}) collective-permute-start(bf16[1040,128]{1,0:T(8,128)(2,1)S(1)} %get-tuple-element.21.own_b), channel_id=1, source_target_pairs={{0,4},{4,8},{8,12},{12,16},{16,20},{20,24},{24,28},{28,32},{32,36}... | collective-permute-start | bytes 798728 | tf_op jit(solution)/shard_map/ppermute | solution.py:418
  41.4 9.0 %collective-permute-start.9 = (bf16[1040,128]{1,0:T(8,128)(2,1)S(1)}, bf16[1040,128]{1,0:T(8,128)(2,1)S(1)}, u32[]{:S(2)}, u32[]{:S(2)}) collective-permute-start(bf16[1040,128]{1,0:T(8,128)(2,1)S(1)} %get-tuple-element.21.own_b), channel_id=1, source_target_pairs={{4,0},{8,4},{12,8},{16,12},{20,16},{24,20},{28,24},{32,28},{36,32}... | collective-permute-start | bytes 798728 | tf_op jit(solution)/shard_map/ppermute | solution.py:418
  46.8 3.6 %copy-start.3 = (s32[4,4]{1,0:T(4,128)S(1)}, s32[4,4]{1,0:T(4,128)}, u32[]{:S(2)}) copy-start(s32[4,4]{1,0:T(4,128)} %qc.1) | copy-start | bytes 196
  53.4 9.1 %collective-permute-start.14 = (bf16[512,128]{1,0:T(8,128)(2,1)S(1)}, bf16[512,128]{1,0:T(8,128)(2,1)S(1)}, u32[]{:S(2)}, u32[]{:S(2)}) collective-permute-start(bf16[512,128]{1,0:T(8,128)(2,1)S(1)} %get-tuple-element.31), channel_id=1, source_target_pairs={{0,1},{1,2},{2,3},{3,0},{4,5},{5,6},{6,7},{7,4},{8,9},{9,10},{10,1... | collective-permute-start | bytes 393224 | tf_op jit(solution)/shard_map/ppermute | solution.py:415
  53.5 9.0 %collective-permute-start.15 = (bf16[512,128]{1,0:T(8,128)(2,1)S(1)}, bf16[512,128]{1,0:T(8,128)(2,1)S(1)}, u32[]{:S(2)}, u32[]{:S(2)}) collective-permute-start(bf16[512,128]{1,0:T(8,128)(2,1)S(1)} %get-tuple-element.32), channel_id=1, source_target_pairs={{0,2},{1,3},{2,0},{3,1},{4,6},{5,7},{6,4},{7,5},{8,10},{9,11},{10,... | collective-permute-start | bytes 393224 | tf_op jit(solution)/shard_map/ppermute | solution.py:415
  55.2 7.4 %collective-permute-start.16 = (bf16[512,128]{1,0:T(8,128)(2,1)S(1)}, bf16[512,128]{1,0:T(8,128)(2,1)S(1)}, u32[]{:S(2)}, u32[]{:S(2)}) collective-permute-start(bf16[512,128]{1,0:T(8,128)(2,1)S(1)} %get-tuple-element.33), channel_id=1, source_target_pairs={{0,3},{1,0},{2,1},{3,2},{4,7},{5,4},{6,5},{7,6},{8,11},{9,8},{10,9... | collective-permute-start | bytes 393224 | tf_op jit(solution)/shard_map/ppermute | solution.py:415

commit v3 on v2

--- a/solution.py
+++ b/solution.py
@@ -73,11 +73,11 @@
     for r in range(rows):
         table = jnp.where(row == r, xc[0, r], table)
     x_high[tail:, :] = table.astype(F32).astype(BF16)
-    for out, start in ((h_up, rows - REACH), (h_down, 0)):
+    for out, start, base in ((h_up, rows - REACH, 0), (h_down, 0, REACH)):
         table = jnp.zeros(shape, I32)
         for r in range(REACH):
             for m in range(slots):
-                table = jnp.where((row == r) & (lane == m), hc[start + r, m], table)
+                table = jnp.where((row == base + r) & (lane == m), hc[start + r, m], table)
         out[edge:, :] = table.astype(F32).astype(BF16)
     for move in moves:
         move.wait()
@@ -108,19 +108,18 @@
     )(*[hbm(a) for a in (x_columns.T, h_columns, x, h)])
 
 
-TABLE = pltpu.VMEM((16, 128), I32)
-
-
-def whole(table, parts):
-    for n, part in enumerate(parts):
-        table[8 * n : 8 * n + 8, :] = part.astype(F32).astype(I32)
+TABLE = pltpu.VMEM((8, 128), I32)
+
+
+def tail(x):
+    return x[x.shape[0] - PAD : x.shape[0] - PAD + 8, :128].astype(F32)
 
 
 def slice_kernel(a_low, a_high, b_low, b_high, out, table):
     d = lax.axis_index("depth")
     tile = pl.ds(pl.multiple_of(d // 2 * 128, 128), 128)
     cut = a_low.shape[0]
-    whole(table, [x[x.shape[0] - PAD : x.shape[0] - PAD + 8, :128] for x in (a_high, b_high)])
+    table[...] = jnp.where(low_half((8, 128)), tail(a_high), tail(b_high)).astype(I32)
     for upper in range(2):
 
         @pl.when(d % 2 == upper)
@@ -145,7 +144,7 @@
 
 def first_slot_kernel(lo, hi, out_lo, out_hi, table):
     size = lo.shape[1]
-    whole(table, [x[x.shape[0] - PAD : x.shape[0] - PAD + 8, :128] for x in (lo, hi)])
+    table[...] = (tail(lo) + tail(hi)).astype(I32)
     step = (lo.shape[0] - PAD) // REACH
     for source, out in ((lo, out_lo), (hi, out_hi)):
         for r in range(REACH):
@@ -205,7 +204,7 @@
         for p in range(slots):
             acc = before[i * slots + p]
             for k in range(1, 4):
-                column = (tab_a, tab_b)[k // 2][8 * (k % 2) + i, 0]
+                column = (tab_a, tab_b)[k // 2][i, 64 * (k % 2)]
                 block = own_block(column, first, all_rows, pc[i, p], hc, h, zero)
                 acc += jnp.dot(x_row(xs, k - 1, i), block, preferred_element_type=F32)
             total[i * slots + p] = acc
@@ -235,13 +234,13 @@
     zero = jnp.zeros((size, size), BF16)
     for i in range(rows):
         far = [(r, lo, lo_side, r, 1, r - REACH) for r in range(REACH) if r - REACH >= i - REACH]
-        far += [(8 + r, hi, hi_side, r, -1, rows + r) for r in range(REACH) if rows + r <= i + REACH]
+        far += [(REACH + r, hi, hi_side, r, -1, rows + r) for r in range(REACH) if rows + r <= i + REACH]
         lefts = []
         for *_, j in far:
             column = lax.rem(first + j + all_rows, all_rows)
             left = zero
             for k in range(4):
-                here = (tab_a, tab_b)[k // 2][8 * (k % 2) + i, 0] == column
+                here = (tab_a, tab_b)[k // 2][i, 64 * (k % 2)] == column
                 left = jnp.where(here, x_row(xs, k, i), left)
             lefts.append(left)
         for p in range(slots):

time: 64.5 us -> 64.5 us (level)
  no operation moved by 1% of the time
where the time goes in v3:
time: 64.5 us; the launch traced here: 63.7 us
  waiting for transfers between devices  26.7 us (41%)
  starting transfers between devices  23.7 us (37%)
  Pallas kernels  12.4 us (19%)
  between operations  0.95 us (1%)
    ppermute x11, waiting for transfers between devices, turn(): lax.ppermute(x, 'depth', [(s, (s + o) % depth) for s in range(depth)])  19.2 us
    ppermute x11, starting transfers between devices, turn(): lax.ppermute(x, 'depth', [(s, (s + o) % depth) for s in range(depth)])  13.7 us
    ppermute x6, starting transfers between devices, shift(): return lax.ppermute(x, ('row', 'col'), pairs)  9.96 us
    ppermute x6, waiting for transfers between devices, shift(): return lax.ppermute(x, ('row', 'col'), pairs)  7.44 us
    pallas_call x2, Pallas kernels, near_terms(): pl.pallas_call(functools.partial(kernel, rows, all_rows), in_specs=[SMEM]...  4.43 us
    pallas_call x1, Pallas kernels, q_product(): pl.pallas_call(functools.partial(q_kernel, rows, all_rows), in_specs=[SME...  2.91 us
    pallas_call x1, Pallas kernels, far_terms(): pl.pallas_call(functools.partial(far_kernel, rows, all_rows), in_specs=[S...  1.98 us
    pallas_call x1, Pallas kernels, pack(): pl.pallas_call(pack_kernel, in_specs=[HBM] * 4, out_specs=[VMEM] * 4, out...  1.78 us
  transfers between devices with their start and end apart: 17, of which 8 were waited for; matrix products, arithmetic and copies ran while one was open for 0% of the time, Pallas kernels for 11%

profile of v3, /device:TPU:7, one launch (start us, length us, event | category | flops | bytes accessed | tf_op | source)
XLA Modules:
  0.0 63.7 jit_solution(6462672513313271648)
XLA Ops:
  0.7 1.8 %pack.1 = (bf16[512,256]{1,0:T(8,128)(2,1)S(1)}, bf16[528,256]{1,0:T(8,128)(2,1)S(1)}, bf16[1552,256]{1,0:T(8,128)(2,1)S(1)}, bf16[1552,256]{1,0:T(8,128)(2,1)S(1)}) custom-call(s32[1,4]{1,0:T(1,128)} %bitcast.12, s32[4,4]{1,0:T(4,128)} %hc.3, bf16[1024,256]{1,0:T(8,128)(2,1)} %bitcast.14, bf16[4096,256]{1,0:T(8,128)(2,1)} %bitcast.9), custom_call_target="tpu_custom_call" | custom-call | tf_op jit(solution)/shard_map/pack/pallas_call | solution.py:91
  2.5 1.7 %collective-permute-start.10 = (bf16[1552,256]{1,0:T(8,128)(2,1)S(1)}, bf16[1552,256]{1,0:T(8,128)(2,1)S(1)}, u32[]{:S(2)}, u32[]{:S(2)}) collective-permute-start(bf16[1552,256]{1,0:T(8,128)(2,1)S(1)} %get-tuple-element.24), channel_id=1, source_target_pairs={{0,4},{4,8},{8,12},{12,16},{16,20},{20,24},{24,28},{28,32},{32,36}... | collective-permute-start | bytes 2383880 | tf_op jit(solution)/shard_map/ppermute | solution.py:417
  4.2 4.6 %collective-permute-start.11 = (bf16[1552,256]{1,0:T(8,128)(2,1)S(1)}, bf16[1552,256]{1,0:T(8,128)(2,1)S(1)}, u32[]{:S(2)}, u32[]{:S(2)}) collective-permute-start(bf16[1552,256]{1,0:T(8,128)(2,1)S(1)} %get-tuple-element.25), channel_id=1, source_target_pairs={{4,0},{8,4},{12,8},{16,12},{20,16},{24,20},{28,24},{32,28},{36,32}... | collective-permute-start | bytes 2383880 | tf_op jit(solution)/shard_map/ppermute | solution.py:417
  8.8 2.7 %collective-permute-start.5 = (bf16[528,256]{1,0:T(8,128)(2,1)S(1)}, bf16[528,256]{1,0:T(8,128)(2,1)S(1)}, u32[]{:S(2)}, u32[]{:S(2)}) collective-permute-start(bf16[528,256]{1,0:T(8,128)(2,1)S(1)} %get-tuple-element.19.a_high.high.refs_1_), channel_id=1, source_target_pairs={{0,3},{1,0},{2,1},{3,2},{4,7},{5,4},{6,5},{7,6},{8,11},{9,8},{10,9... | collective-permute-start | bytes 811016 | tf_op jit(solution)/shard_map/ppermute | solution.py:414
  11.5 5.7 %collective-permute-done.5.a_high.refs_3_.refs_5_ = bf16[528,256]{1,0:T(8,128)(2,1)S(1)} collective-permute-done((bf16[528,256]{1,0:T(8,128)(2,1)S(1)}, bf16[528,256]{1,0:T(8,128)(2,1)S(1)}, u32[]{:S(2)}, u32[]{:S(2)}) %collective-permute-start.5) | collective-permute-done | bytes 270368 | tf_op jit(solution)/shard_map/ppermute | solution.py:414
  17.3 3.4 %collective-permute-start.7 = (bf16[528,256]{1,0:T(8,128)(2,1)S(1)}, bf16[528,256]{1,0:T(8,128)(2,1)S(1)}, u32[]{:S(2)}, u32[]{:S(2)}) collective-permute-start(bf16[528,256]{1,0:T(8,128)(2,1)S(1)} %collective-permute-done.5.a_high.refs_3_.refs_5_), channel_id=1, source_target_pairs={{0,3},{1,0},{2,1},{3,2},{4,7},{5,4},{6,5},{7,6},{8,11},{9,8},{10,9... | collective-permute-start | bytes 811016 | tf_op jit(solution)/shard_map/ppermute | solution.py:414
  20.7 5.7 %collective-permute-done.10.lo.refs_8_ = bf16[1552,256]{1,0:T(8,128)(2,1)S(1)} collective-permute-done((bf16[1552,256]{1,0:T(8,128)(2,1)S(1)}, bf16[1552,256]{1,0:T(8,128)(2,1)S(1)}, u32[]{:S(2)}, u32[]{:S(2)}) %collective-permute-start.10) | collective-permute-done | bytes 794656 | tf_op jit(solution)/shard_map/ppermute | solution.py:417
  26.4 1.0 %collective-permute-start.6 = (bf16[512,256]{1,0:T(8,128)(2,1)S(1)}, bf16[512,256]{1,0:T(8,128)(2,1)S(1)}, u32[]{:S(2)}, u32[]{:S(2)}) collective-permute-start(bf16[512,256]{1,0:T(8,128)(2,1)S(1)} %collective-permute-done.b_low.refs_0_.refs_2_), channel_id=1, source_target_pairs={{0,1},{1,2},{2,3},{3,0},{4,5},{5,6},{6,7},{7,4},{8,9},{9,10},{10,1... | collective-permute-start | bytes 786440 | tf_op jit(solution)/shard_map/ppermute | solution.py:414
  27.4 1.4 %collective-permute-start.12 = (bf16[512,256]{1,0:T(8,128)(2,1)S(1)}, bf16[512,256]{1,0:T(8,128)(2,1)S(1)}, u32[]{:S(2)}, u32[]{:S(2)}) collective-permute-start(bf16[512,256]{1,0:T(8,128)(2,1)S(1)} %get-tuple-element.27), channel_id=1, source_target_pairs={{0,1},{1,2},{2,3},{3,0},{4,5},{5,6},{6,7},{7,4},{8,9},{9,10},{10,1... | collective-permute-start | bytes 786440 | tf_op jit(solution)/shard_map/ppermute | solution.py:414
  28.8 1.4 %collective-permute-start.13 = (bf16[512,256]{1,0:T(8,128)(2,1)S(1)}, bf16[512,256]{1,0:T(8,128)(2,1)S(1)}, u32[]{:S(2)}, u32[]{:S(2)}) collective-permute-start(bf16[512,256]{1,0:T(8,128)(2,1)S(1)} %get-tuple-element.28), channel_id=1, source_target_pairs={{0,3},{1,0},{2,1},{3,2},{4,7},{5,4},{6,5},{7,6},{8,11},{9,8},{10,9... | collective-permute-start | bytes 786440 | tf_op jit(solution)/shard_map/ppermute | solution.py:414
  30.4 0.8 %collective-permute-done.4.a_low.refs_2_.refs_4_ = bf16[512,256]{1,0:T(8,128)(2,1)S(1)} collective-permute-done((bf16[512,256]{1,0:T(8,128)(2,1)S(1)}, bf16[512,256]{1,0:T(8,128)(2,1)S(1)}, u32[]{:S(2)}, u32[]{:S(2)}) %collective-permute-start.4) | collective-permute-done | bytes 262176 | tf_op jit(solution)/shard_map/ppermute | solution.py:414
  31.2 4.6 %collective-permute-done.6.b_low.refs_4_.refs_6_ = bf16[512,256]{1,0:T(8,128)(2,1)S(1)} collective-permute-done((bf16[512,256]{1,0:T(8,128)(2,1)S(1)}, bf16[512,256]{1,0:T(8,128)(2,1)S(1)}, u32[]{:S(2)}, u32[]{:S(2)}) %collective-permute-start.6) | collective-permute-done | bytes 262176 | tf_op jit(solution)/shard_map/ppermute | solution.py:414
  35.8 2.7 %collective-permute-start.3 = (bf16[1040,128]{1,0:T(8,128)(2,1)S(1)}, bf16[1040,128]{1,0:T(8,128)(2,1)S(1)}, u32[]{:S(2)}, u32[]{:S(2)}) collective-permute-start(bf16[1040,128]{1,0:T(8,128)(2,1)S(1)} %get-tuple-element.20.own_a), channel_id=1, source_target_pairs={{4,0},{8,4},{12,8},{16,12},{20,16},{24,20},{28,24},{32,28},{36,32}... | collective-permute-start | bytes 798728 | tf_op jit(solution)/shard_map/ppermute | solution.py:417
  38.8 2.6 %collective-permute-done.12.refs_10_ = bf16[512,256]{1,0:T(8,128)(2,1)S(1)} collective-permute-done((bf16[512,256]{1,0:T(8,128)(2,1)S(1)}, bf16[512,256]{1,0:T(8,128)(2,1)S(1)}, u32[]{:S(2)}, u32[]{:S(2)}) %collective-permute-start.12) | collective-permute-done | bytes 262176 | tf_op jit(solution)/shard_map/ppermute | solution.py:414
  41.4 0.8 %collective-permute-start.9 = (bf16[1040,128]{1,0:T(8,128)(2,1)S(1)}, bf16[1040,128]{1,0:T(8,128)(2,1)S(1)}, u32[]{:S(2)}, u32[]{:S(2)}) collective-permute-start(bf16[1040,128]{1,0:T(8,128)(2,1)S(1)} %get-tuple-element.21.own_b), channel_id=1, source_target_pairs={{4,0},{8,4},{12,8},{16,12},{20,16},{24,20},{28,24},{32,28},{36,32}... | collective-permute-start | bytes 798728 | tf_op jit(solution)/shard_map/ppermute | solution.py:417
  42.2 1.5 %shard_map.77.refs_7_ = f32[16,256,256]{2,1,0:T(8,128)S(1)} custom-call(s32[4,4]{1,0:T(4,128)S(1)} %copy-done.1, s32[4,4]{1,0:T(4,128)S(1)} %copy-done.2, s32[1,4]{1,0:T(1,128)S(1)} %bitcast.13, bf16[512,256]{1,0:T(8,128)(2,1)S(1)} %get-tuple-element.18.a_low.low.refs_0_, bf16[528,256]{1,0:T(8,128)(2,1)S(1)} %get-tuple-element.19.a_high.high.refs_1_, ...), custom_call_target="tpu_custom_call" | custom-call | flops 536870912 | bytes 9437184 | tf_op jit(solution)/shard_map/pallas_call | solution.py:217
  43.7 2.9 %shard_map.78.refs_12_ = f32[16,256,256]{2,1,0:T(8,128)S(1)} custom-call(s32[4,4]{1,0:T(4,128)S(1)} %copy-done.1, s32[4,4]{1,0:T(4,128)S(1)} %copy-done.2, s32[8,128]{1,0:T(8,128)S(1)} %get-tuple-element.22.tab_a, s32[8,128]{1,0:T(8,128)S(1)} %get-tuple-element.23.tab_b, bf16[512,256]{1,0:T(8,128)(2,1)S(1)} %collective-permute-done.b_low.refs_0_.refs_2_, ...), custom_call_target="tpu_custom_call" | custom-call | flops 1610612736 | bytes 9437184 | tf_op jit(solution)/shard_map/pallas_call | solution.py:217
  46.7 2.0 %far_terms.1.full = bf16[16,256,256]{2,1,0:T(8,128)(2,1)S(1)} custom-call(s32[4,4]{1,0:T(4,128)S(1)} %copy-done.1, s32[8,128]{1,0:T(8,128)S(1)} %get-tuple-element.22.tab_a, s32[8,128]{1,0:T(8,128)S(1)} %get-tuple-element.23.tab_b, s32[8,128]{1,0:T(8,128)S(1)} %get-tuple-element.26.tab_h, bf16[512,256]{1,0:T(8,128)(2,1)S(1)} %get-tuple-element.18.a_low.low.refs_0_, ...), custom_call_target="tpu_custom_call" | custom-call | flops 805306368 | bytes 9437184 | tf_op jit(solution)/shard_map/far_terms/pallas_call | solution.py:269
  48.7 1.7 %collective-permute-done.9.hi_b = bf16[1040,128]{1,0:T(8,128)(2,1)S(1)} collective-permute-done((bf16[1040,128]{1,0:T(8,128)(2,1)S(1)}, bf16[1040,128]{1,0:T(8,128)(2,1)S(1)}, u32[]{:S(2)}, u32[]{:S(2)}) %collective-permute-start.9) | collective-permute-done | bytes 266272 | tf_op jit(solution)/shard_map/ppermute | solution.py:417
  50.4 2.9 %q_product.1 = (bf16[512,128]{1,0:T(8,128)(2,1)S(1)}, bf16[512,128]{1,0:T(8,128)(2,1)S(1)}, bf16[512,128]{1,0:T(8,128)(2,1)S(1)}, bf16[512,128]{1,0:T(8,128)(2,1)S(1)}, bf16[4,256,256]{2,1,0:T(8,128)(2,1)}) custom-call(s32[4,4]{1,0:T(4,128)S(1)} %copy-done.1, s32[4,4]{1,0:T(4,128)S(1)} %copy-done.3, bf16[1040,128]{1,0:T(8,128)(2,1)S(1)} %collective-permute-done.2.lo_a, ...), custom_call_target="tpu_custom_call" | custom-call | flops 536870912 | bytes 5242880 | tf_op jit(solution)/shard_map/q_product/pallas_call | solution.py:344
  53.5 1.7 %collective-permute-start.15 = (bf16[512,128]{1,0:T(8,128)(2,1)S(1)}, bf16[512,128]{1,0:T(8,128)(2,1)S(1)}, u32[]{:S(2)}, u32[]{:S(2)}) collective-permute-start(bf16[512,128]{1,0:T(8,128)(2,1)S(1)} %get-tuple-element.32), channel_id=1, source_target_pairs={{0,2},{1,3},{2,0},{3,1},{4,6},{5,7},{6,4},{7,5},{8,10},{9,11},{10,... | collective-permute-start | bytes 393224 | tf_op jit(solution)/shard_map/ppermute | solution.py:414
  55.2 2.0 %collective-permute-start.16 = (bf16[512,128]{1,0:T(8,128)(2,1)S(1)}, bf16[512,128]{1,0:T(8,128)(2,1)S(1)}, u32[]{:S(2)}, u32[]{:S(2)}) collective-permute-start(bf16[512,128]{1,0:T(8,128)(2,1)S(1)} %get-tuple-element.33), channel_id=1, source_target_pairs={{0,3},{1,0},{2,1},{3,2},{4,7},{5,4},{6,5},{7,6},{8,11},{9,8},{10,9... | collective-permute-start | bytes 393224 | tf_op jit(solution)/shard_map/ppermute | solution.py:414
  57.1 5.3 %collective-permute-done.14.t1 = bf16[512,128]{1,0:T(8,128)(2,1)S(1)} collective-permute-done((bf16[512,128]{1,0:T(8,128)(2,1)S(1)}, bf16[512,128]{1,0:T(8,128)(2,1)S(1)}, u32[]{:S(2)}, u32[]{:S(2)}) %collective-permute-start.14) | collective-permute-done | bytes 131104 | tf_op jit(solution)/shard_map/ppermute | solution.py:414
  62.6 1.0 %join.1 = bf16[4,256,256]{2,1,0:T(8,128)(2,1)} custom-call(bf16[512,128]{1,0:T(8,128)(2,1)S(1)} %get-tuple-element.30.t0, bf16[512,128]{1,0:T(8,128)(2,1)S(1)} %collective-permute-done.14.t1, bf16[512,128]{1,0:T(8,128)(2,1)S(1)} %collective-permute-done.15.t2, bf16[512,128]{1,0:T(8,128)(2,1)S(1)} %collective-permute-done.16.t3), custom_call_target="tpu_custom_call" | custom-call | tf_op jit(solution)/shard_map/join/pallas_call | solution.py:390
  (29 shorter events, 0.7 us)
Async XLA Ops:
  0.6 41.6 %copy-start = (bf16[4,4,256,256]{3,2,1,0:T(8,128)(2,1)S(1)}, bf16[4,4,256,256]{3,2,1,0:T(8,128)(2,1)}, u32[]{:S(2)}) copy-start(bf16[4,4,256,256]{3,2,1,0:T(8,128)(2,1)} %param.8) | copy-start | bytes 6291460
  0.6 41.6 %copy-start.4 = (s32[4,1]{0,1:T(1,128)S(1)}, s32[4,1]{0,1:T(1,128)}, u32[]{:S(2)}) copy-start(s32[4,1]{0,1:T(1,128)} %param.7) | copy-start | bytes 52
  0.7 41.6 %copy-start.2 = (s32[4,4]{1,0:T(4,128)S(1)}, s32[4,4]{1,0:T(4,128)}, u32[]{:S(2)}) copy-start(s32[4,4]{1,0:T(4,128)} %hc.3) | copy-start | bytes 196
  0.7 41.6 %copy-start.1 = (s32[4,4]{1,0:T(4,128)S(1)}, s32[4,4]{1,0:T(4,128)}, u32[]{:S(2)}) copy-start(s32[4,4]{1,0:T(4,128)} %pc.7) | copy-start | bytes 196
  2.5 23.9 %collective-permute-start.10 = (bf16[1552,256]{1,0:T(8,128)(2,1)S(1)}, bf16[1552,256]{1,0:T(8,128)(2,1)S(1)}, u32[]{:S(2)}, u32[]{:S(2)}) collective-permute-start(bf16[1552,256]{1,0:T(8,128)(2,1)S(1)} %get-tuple-element.24), channel_id=1, source_target_pairs={{0,4},{4,8},{8,12},{12,16},{16,20},{20,24},{24,28},{28,32},{32,36}... | collective-permute-start | bytes 2383880 | tf_op jit(solution)/shard_map/ppermute | solution.py:417
  4.2 23.2 %collective-permute-start.11 = (bf16[1552,256]{1,0:T(8,128)(2,1)S(1)}, bf16[1552,256]{1,0:T(8,128)(2,1)S(1)}, u32[]{:S(2)}, u32[]{:S(2)}) collective-permute-start(bf16[1552,256]{1,0:T(8,128)(2,1)S(1)} %get-tuple-element.25), channel_id=1, source_target_pairs={{4,0},{8,4},{12,8},{16,12},{20,16},{24,20},{28,24},{32,28},{36,32}... | collective-permute-start | bytes 2383880 | tf_op jit(solution)/shard_map/ppermute | solution.py:417
  8.8 8.5 %collective-permute-start.5 = (bf16[528,256]{1,0:T(8,128)(2,1)S(1)}, bf16[528,256]{1,0:T(8,128)(2,1)S(1)}, u32[]{:S(2)}, u32[]{:S(2)}) collective-permute-start(bf16[528,256]{1,0:T(8,128)(2,1)S(1)} %get-tuple-element.19.a_high.high.refs_1_), channel_id=1, source_target_pairs={{0,3},{1,0},{2,1},{3,2},{4,7},{5,4},{6,5},{7,6},{8,11},{9,8},{10,9... | collective-permute-start | bytes 811016 | tf_op jit(solution)/shard_map/ppermute | solution.py:414
  11.5 9.2 %collective-permute-start = (bf16[512,256]{1,0:T(8,128)(2,1)S(1)}, bf16[512,256]{1,0:T(8,128)(2,1)S(1)}, u32[]{:S(2)}, u32[]{:S(2)}) collective-permute-start(bf16[512,256]{1,0:T(8,128)(2,1)S(1)} %get-tuple-element.18.a_low.low.refs_0_), channel_id=1, source_target_pairs={{0,1},{1,2},{2,3},{3,0},{4,5},{5,6},{6,7},{7,4},{8,9},{9,10},{10,1... | collective-permute-start | bytes 786440 | tf_op jit(solution)/shard_map/ppermute | solution.py:414
  11.5 17.3 %collective-permute-start.1 = (bf16[528,256]{1,0:T(8,128)(2,1)S(1)}, bf16[528,256]{1,0:T(8,128)(2,1)S(1)}, u32[]{:S(2)}, u32[]{:S(2)}) collective-permute-start(bf16[528,256]{1,0:T(8,128)(2,1)S(1)} %get-tuple-element.19.a_high.high.refs_1_), channel_id=1, source_target_pairs={{0,1},{1,2},{2,3},{3,0},{4,5},{5,6},{6,7},{7,4},{8,9},{9,10},{10,1... | collective-permute-start | bytes 811016 | tf_op jit(solution)/shard_map/ppermute | solution.py:414
  17.3 21.3 %collective-permute-start.7 = (bf16[528,256]{1,0:T(8,128)(2,1)S(1)}, bf16[528,256]{1,0:T(8,128)(2,1)S(1)}, u32[]{:S(2)}, u32[]{:S(2)}) collective-permute-start(bf16[528,256]{1,0:T(8,128)(2,1)S(1)} %collective-permute-done.5.a_high.refs_3_.refs_5_), channel_id=1, source_target_pairs={{0,3},{1,0},{2,1},{3,2},{4,7},{5,4},{6,5},{7,6},{8,11},{9,8},{10,9... | collective-permute-start | bytes 811016 | tf_op jit(solution)/shard_map/ppermute | solution.py:414
  20.7 10.5 %collective-permute-start.4 = (bf16[512,256]{1,0:T(8,128)(2,1)S(1)}, bf16[512,256]{1,0:T(8,128)(2,1)S(1)}, u32[]{:S(2)}, u32[]{:S(2)}) collective-permute-start(bf16[512,256]{1,0:T(8,128)(2,1)S(1)} %get-tuple-element.18.a_low.low.refs_0_), channel_id=1, source_target_pairs={{0,3},{1,0},{2,1},{3,2},{4,7},{5,4},{6,5},{7,6},{8,11},{9,8},{10,9... | collective-permute-start | bytes 786440 | tf_op jit(solution)/shard_map/ppermute | solution.py:414
  26.4 9.4 %collective-permute-start.6 = (bf16[512,256]{1,0:T(8,128)(2,1)S(1)}, bf16[512,256]{1,0:T(8,128)(2,1)S(1)}, u32[]{:S(2)}, u32[]{:S(2)}) collective-permute-start(bf16[512,256]{1,0:T(8,128)(2,1)S(1)} %collective-permute-done.b_low.refs_0_.refs_2_), channel_id=1, source_target_pairs={{0,1},{1,2},{2,3},{3,0},{4,5},{5,6},{6,7},{7,4},{8,9},{9,10},{10,1... | collective-permute-start | bytes 786440 | tf_op jit(solution)/shard_map/ppermute | solution.py:414
  27.4 14.0 %collective-permute-start.12 = (bf16[512,256]{1,0:T(8,128)(2,1)S(1)}, bf16[512,256]{1,0:T(8,128)(2,1)S(1)}, u32[]{:S(2)}, u32[]{:S(2)}) collective-permute-start(bf16[512,256]{1,0:T(8,128)(2,1)S(1)} %get-tuple-element.27), channel_id=1, source_target_pairs={{0,1},{1,2},{2,3},{3,0},{4,5},{5,6},{6,7},{7,4},{8,9},{9,10},{10,1... | collective-permute-start | bytes 786440 | tf_op jit(solution)/shard_map/ppermute | solution.py:414
  28.8 17.9 %collective-permute-start.13 = (bf16[512,256]{1,0:T(8,128)(2,1)S(1)}, bf16[512,256]{1,0:T(8,128)(2,1)S(1)}, u32[]{:S(2)}, u32[]{:S(2)}) collective-permute-start(bf16[512,256]{1,0:T(8,128)(2,1)S(1)} %get-tuple-element.28), channel_id=1, source_target_pairs={{0,3},{1,0},{2,1},{3,2},{4,7},{5,4},{6,5},{7,6},{8,11},{9,8},{10,9... | collective-permute-start | bytes 786440 | tf_op jit(solution)/shard_map/ppermute | solution.py:414
  31.2 17.5 %collective-permute-start.2 = (bf16[1040,128]{1,0:T(8,128)(2,1)S(1)}, bf16[1040,128]{1,0:T(8,128)(2,1)S(1)}, u32[]{:S(2)}, u32[]{:S(2)}) collective-permute-start(bf16[1040,128]{1,0:T(8,128)(2,1)S(1)} %get-tuple-element.20.own_a), channel_id=1, source_target_pairs={{0,4},{4,8},{8,12},{12,16},{16,20},{20,24},{24,28},{28,32},{32,36}... | collective-permute-start | bytes 798728 | tf_op jit(solution)/shard_map/ppermute | solution.py:417
  35.8 12.9 %collective-permute-start.3 = (bf16[1040,128]{1,0:T(8,128)(2,1)S(1)}, bf16[1040,128]{1,0:T(8,128)(2,1)S(1)}, u32[]{:S(2)}, u32[]{:S(2)}) collective-permute-start(bf16[1040,128]{1,0:T(8,128)(2,1)S(1)} %get-tuple-element.20.own_a), channel_id=1, source_target_pairs={{4,0},{8,4},{12,8},{16,12},{20,16},{24,20},{28,24},{32,28},{36,32}... | collective-permute-start | bytes 798728 | tf_op jit(solution)/shard_map/ppermute | solution.py:417
  38.7 10.0 %collective-permute-start.8 = (bf16[1040,128]{1,0:T(8,128)(2,1)S(1)}, bf16[1040,128]{1,0:T(8,128)(2,1)S(1)}, u32[]{:S(2)}, u32[]{:S(2)}) collective-permute-start(bf16[1040,128]{1,0:T(8,128)(2,1)S(1)} %get-tuple-element.21.own_b), channel_id=1, source_target_pairs={{0,4},{4,8},{8,12},{12,16},{16,20},{20,24},{24,28},{28,32},{32,36}... | collective-permute-start | bytes 798728 | tf_op jit(solution)/shard_map/ppermute | solution.py:417
  41.4 9.0 %collective-permute-start.9 = (bf16[1040,128]{1,0:T(8,128)(2,1)S(1)}, bf16[1040,128]{1,0:T(8,128)(2,1)S(1)}, u32[]{:S(2)}, u32[]{:S(2)}) collective-permute-start(bf16[1040,128]{1,0:T(8,128)(2,1)S(1)} %get-tuple-element.21.own_b), channel_id=1, source_target_pairs={{4,0},{8,4},{12,8},{16,12},{20,16},{24,20},{28,24},{32,28},{36,32}... | collective-permute-start | bytes 798728 | tf_op jit(solution)/shard_map/ppermute | solution.py:417
  46.7 3.8 %copy-start.3 = (s32[4,4]{1,0:T(4,128)S(1)}, s32[4,4]{1,0:T(4,128)}, u32[]{:S(2)}) copy-start(s32[4,4]{1,0:T(4,128)} %qc.1) | copy-start | bytes 196
  53.4 9.1 %collective-permute-start.14 = (bf16[512,128]{1,0:T(8,128)(2,1)S(1)}, bf16[512,128]{1,0:T(8,128)(2,1)S(1)}, u32[]{:S(2)}, u32[]{:S(2)}) collective-permute-start(bf16[512,128]{1,0:T(8,128)(2,1)S(1)} %get-tuple-element.31), channel_id=1, source_target_pairs={{0,1},{1,2},{2,3},{3,0},{4,5},{5,6},{6,7},{7,4},{8,9},{9,10},{10,1... | collective-permute-start | bytes 393224 | tf_op jit(solution)/shard_map/ppermute | solution.py:414
  53.5 9.0 %collective-permute-start.15 = (bf16[512,128]{1,0:T(8,128)(2,1)S(1)}, bf16[512,128]{1,0:T(8,128)(2,1)S(1)}, u32[]{:S(2)}, u32[]{:S(2)}) collective-permute-start(bf16[512,128]{1,0:T(8,128)(2,1)S(1)} %get-tuple-element.32), channel_id=1, source_target_pairs={{0,2},{1,3},{2,0},{3,1},{4,6},{5,7},{6,4},{7,5},{8,10},{9,11},{10,... | collective-permute-start | bytes 393224 | tf_op jit(solution)/shard_map/ppermute | solution.py:414
  55.2 7.4 %collective-permute-start.16 = (bf16[512,128]{1,0:T(8,128)(2,1)S(1)}, bf16[512,128]{1,0:T(8,128)(2,1)S(1)}, u32[]{:S(2)}, u32[]{:S(2)}) collective-permute-start(bf16[512,128]{1,0:T(8,128)(2,1)S(1)} %get-tuple-element.33), channel_id=1, source_target_pairs={{0,3},{1,0},{2,1},{3,2},{4,7},{5,4},{6,5},{7,6},{8,11},{9,8},{10,9... | collective-permute-start | bytes 393224 | tf_op jit(solution)/shard_map/ppermute | solution.py:414
